TPU v7x, 512 devices: a whole 4x8x8 slice. The times are simulated.
512 devices in a mesh: gx: 16 (over y, core), gz: 16 (over x, z_lo), grp: 2 (over z_hi).
Axes of the slice: x: 4, y: 8, z: 8 (z_hi: 2, z_lo: 4; z = z_hi * 4 + z_lo), core: 2. Of those that a mesh axis runs over, the one named last changes fastest.
Arguments:
- velocity: float32 [3, 3, 512, 2048], P(None, None, ('gz', 'grp'), 'gx'), may hold values from -5 to 5
- slab_average_downflow_speed: float32 [3], replicated, may hold values from 0.5 to 2
- mean_shear: float32 [3], replicated, may hold values from -2 to 2
- mode_counts: int32 [3, 2], replicated, may hold values from 64 to 128
Outputs:
- advanced: float32 [3, 3, 512, 2048], P(None, None, ('gz', 'grp'), 'gx')
- stress: float32 [6, 3, 512, 2048], P(None, None, ('gz', 'grp'), 'gx')
All inputs are finite; a program needn't handle non-finite values.
Results may differ from a plain program's by a relative error of at most 0.00015.
Values sent between devices are 32-bit elements; how exact they have to be, the bound alone decides.
No kernel may reach another device: no remote copies, remote signals or barrier semaphores. Data moves between devices by JAX's collectives and lax.ppermute only.
A program may use at most 64 MiB of HBM per device.

v0:
```python
import math

import jax
import jax.numpy as jnp
from jax import lax
from jax.sharding import PartitionSpec as P

NX = 2048
NZ = 512
MODES = 256


molecular_diffusivity = 0.4
time_step = 0.2
highest = lax.Precision.HIGHEST
pair_first = (0, 0, 0, 1, 1, 2)
pair_second = (0, 1, 2, 1, 2, 2)


def with_halo(cells, sides, width):
    for axis, dim in sides:
        count = lax.axis_size(axis)
        head = lax.slice_in_dim(cells, 0, width, axis=dim)
        tail = lax.slice_in_dim(cells, cells.shape[dim] - width, cells.shape[dim], axis=dim)
        cells = jnp.concatenate(
            [
                lax.ppermute(tail, axis, [(i, (i + 1) % count) for i in range(count)]),
                cells,
                lax.ppermute(head, axis, [((i + 1) % count, i) for i in range(count)]),
            ],
            axis=dim,
        )
    return cells


def split_up(shard, dim, count):
    shape = shard.shape
    tiles = shard.reshape(*shape[:dim], count, shape[dim] // count, *shape[dim + 1 :])
    return jnp.moveaxis(tiles, dim, 0)


def summed_on_arrival(shard, axis, dim):
    count = lax.axis_size(axis)
    tiles = lax.all_to_all(split_up(shard, dim, count), axis, 0, 0, tiled=True)
    return jnp.sum(tiles, axis=0)


def copy_for_each(shard, axis):
    copies = jnp.broadcast_to(shard, (lax.axis_size(axis), *shard.shape))
    return lax.all_to_all(copies, axis, split_axis=0, concat_axis=0, tiled=True)


def joined_along(tiles, dim):
    tiles = jnp.moveaxis(tiles, 0, dim)
    shape = tiles.shape
    return tiles.reshape(*shape[:dim], shape[dim] * shape[dim + 1], *shape[dim + 2 :])


def collect(shard, axis, dim):
    tiles = copy_for_each(shard, axis)
    return joined_along(tiles, dim)


def wave_numbers(modes):
    column = jnp.arange(modes, dtype=jnp.int32)
    half_modes = modes // 2
    return jnp.where(column < half_modes, column, column - half_modes + 1)


def wave_table(positions, length, modes):
    column = jnp.arange(modes, dtype=jnp.int32)
    numbers = wave_numbers(modes)
    phase_int = positions[:, None] * numbers[None, :] % length
    angles = phase_int.astype(jnp.float32) * jnp.float32(2.0 * math.pi / length)
    return jnp.where(column[None, :] < modes // 2, jnp.cos(angles), jnp.sin(angles))


def mode_weights(length, modes):
    column = jnp.arange(modes, dtype=jnp.int32)
    return jnp.where(column == 0, jnp.float32(1.0 / length), jnp.float32(2.0 / length))


def tendency_from(
    middle_entry,
    east_cells,
    west_cells,
    north_cells,
    south_cells,
    slab_average_downflow_speed,
    mean_shear,
):
    downflow_derivative_field = (east_cells - west_cells) * 0.5
    crossflow_derivative_field = (north_cells - south_cells) * 0.5
    diffusion_contribution = (
        east_cells + west_cells + north_cells + south_cells - 4.0 * middle_entry
    )
    holding_slab = slab_average_downflow_speed[:, None, None] + middle_entry[0]
    advanced_state = (
        -holding_slab[None] * downflow_derivative_field
        - middle_entry[2][None] * crossflow_derivative_field
        + molecular_diffusivity * diffusion_contribution
    )
    shear_term = mean_shear[:, None, None] * middle_entry[1]
    return jnp.concatenate([advanced_state[0:1] - shear_term[None], advanced_state[1:]], axis=0)


def with_products(components):
    products = [
        components[first_idx] * components[second_idx]
        for first_idx, second_idx in zip(pair_first, pair_second)
    ]
    return jnp.concatenate([components, jnp.stack(products)], axis=0)


def inner_part(field, margin):
    return field[:, :, margin : field.shape[2] - margin, margin : field.shape[3] - margin]


def padded_rate(padded, slab_average_downflow_speed, mean_shear):
    return tendency_from(
        padded[:, :, 1:-1, 1:-1],
        padded[:, :, 1:-1, 2:],
        padded[:, :, 1:-1, :-2],
        padded[:, :, 2:, 1:-1],
        padded[:, :, :-2, 1:-1],
        slab_average_downflow_speed,
        mean_shear,
    )


def local(velocity, slab_average_downflow_speed, mean_shear, mode_counts):
    cells_z = velocity.shape[2]
    cells_x = velocity.shape[3]
    extended = with_halo(velocity, ((("gz", "grp"), 2), ("gx", 3)), 3)
    first = inner_part(extended, 1) + time_step * padded_rate(
        extended, slab_average_downflow_speed, mean_shear
    )
    second = 0.75 * inner_part(extended, 2) + 0.25 * (
        inner_part(first, 1)
        + time_step * padded_rate(first, slab_average_downflow_speed, mean_shear)
    )
    advanced = inner_part(extended, 3) / 3.0 + 2.0 / 3.0 * (
        inner_part(second, 1)
        + time_step * padded_rate(second, slab_average_downflow_speed, mean_shear)
    )
    streamwise_devices = lax.axis_size("gx")
    spanwise_devices = lax.axis_size(("gz", "grp"))
    modes_x_local = MODES // streamwise_devices
    modes_z_local = MODES // spanwise_devices
    x_positions = lax.axis_index("gx") * cells_x + jnp.arange(cells_x, dtype=jnp.int32)
    z_positions = lax.axis_index(("gz", "grp")) * cells_z + jnp.arange(cells_z, dtype=jnp.int32)
    synth_x = wave_table(x_positions, NX, MODES)
    synth_z = wave_table(z_positions, NZ, MODES)
    analysis_z = synth_z * mode_weights(NZ, MODES)[None, :]
    tile_fields = with_products(advanced)
    analysis_x = synth_x * mode_weights(NX, MODES)[None, :]
    columns = analysis_x
    streamwise = summed_on_arrival(
        jnp.einsum("fpzx,xm->mfpz", tile_fields, columns, precision=highest), "gx", 0
    )
    columns = analysis_z
    spectral = summed_on_arrival(
        jnp.einsum("mfpz,zn->nmfp", streamwise, columns, precision=highest), ("gz", "grp"), 0
    )
    numbers = wave_numbers(MODES)
    z_modes = lax.axis_index(("gz", "grp")) * modes_z_local + jnp.arange(
        modes_z_local, dtype=jnp.int32
    )
    x_modes = lax.axis_index("gx") * modes_x_local + jnp.arange(modes_x_local, dtype=jnp.int32)
    keep_z = jnp.take(numbers, z_modes)[:, None] <= mode_counts[:, 1][None, :]
    keep_x = jnp.take(numbers, x_modes)[:, None] <= mode_counts[:, 0][None, :]
    keep = (keep_z[:, None, :] & keep_x[None, :, :]).astype(jnp.float32)
    spectral = spectral * keep[:, :, None, :]
    columns = synth_z
    partial_sum = jnp.einsum(
        "nmfp,zn->mfpz", collect(spectral, ("gz", "grp"), 0), columns, precision=highest
    )
    columns = synth_x
    filtered = jnp.einsum(
        "mfpz,xm->fpzx", collect(partial_sum, "gx", 0), columns, precision=highest
    )
    stresses = [
        filtered[3 + index] - filtered[first_idx] * filtered[second_idx]
        for index, (first_idx, second_idx) in enumerate(zip(pair_first, pair_second))
    ]
    return (advanced, jnp.stack(stresses))


def solution(mesh):
    return jax.shard_map(
        local,
        mesh=mesh,
        in_specs=(P(None, None, ("gz", "grp"), "gx"), P(), P(), P()),
        out_specs=(P(None, None, ("gz", "grp"), "gx"), P(None, None, ("gz", "grp"), "gx")),
        check_vma=False,
    )
```

profile of v0, /device:TPU:1, one launch (start us, length us, event | category | flops | bytes accessed | tf_op | source)
XLA Modules:
  0.0 176.0 jit_solution(4925099942777690909)
XLA Ops:
  0.7 0.8 fusion.97
  1.5 11.4 %collective-permute-start = (f32[3,3,3,128]{3,2,1,0:T(4,128)S(1)}, f32[3,3,3,128]{3,2,1,0:T(4,128)S(1)}, u32[]{:S(2)}, u32[]{:S(2)}) collective-permute-start(f32[3,3,3,128]{3,2,1,0:T(4,128)S(1)} %get-tuple-element.12), channel_id=1, source_target_pairs={{0,1},{1,2},{2,3},{3,4},{4,5},{5,6},{6,7},{7,8},{8,9},{9,10},{10,1... | collective-permute-start | bytes 41480 | tf_op jit(solution)/shard_map/ppermute | solution.py:27
  12.9 4.1 %collective-permute-start.1 = (f32[3,3,3,128]{3,2,1,0:T(4,128)S(1)}, f32[3,3,3,128]{3,2,1,0:T(4,128)S(1)}, u32[]{:S(2)}, u32[]{:S(2)}) collective-permute-start(f32[3,3,3,128]{3,2,1,0:T(4,128)S(1)} %get-tuple-element.13), channel_id=1, source_target_pairs={{1,0},{2,1},{3,2},{4,3},{5,4},{6,5},{7,6},{8,7},{9,8},{10,9},{11,1... | collective-permute-start | bytes 41480 | tf_op jit(solution)/shard_map/ppermute | solution.py:29
  17.2 4.5 %collective-permute-done.1 = f32[3,3,3,128]{3,2,1,0:T(4,128)S(1)} collective-permute-done((f32[3,3,3,128]{3,2,1,0:T(4,128)S(1)}, f32[3,3,3,128]{3,2,1,0:T(4,128)S(1)}, u32[]{:S(2)}, u32[]{:S(2)}) %collective-permute-start.1) | collective-permute-done | bytes 13856 | tf_op jit(solution)/shard_map/ppermute | solution.py:29
  21.7 0.9 pad_maximum_fusion.1
  22.7 3.1 %collective-permute-start.2 = (f32[3,3,22,3]{3,2,1,0:T(8,128)S(1)}, f32[3,3,22,3]{3,2,1,0:T(8,128)S(1)}, u32[]{:S(2)}, u32[]{:S(2)}) collective-permute-start(f32[3,3,22,3]{3,2,1,0:T(8,128)S(1)} %get-tuple-element.10), channel_id=1, source_target_pairs={{0,32},{32,64},{64,96},{96,128},{128,160},{160,192},{192,224},{224... | collective-permute-start | bytes 7136 | tf_op jit(solution)/shard_map/ppermute | solution.py:27
  25.8 1.7 collective-permute-done.2
  27.5 2.4 %collective-permute-done.3 = f32[3,3,22,3]{3,2,1,0:T(8,128)S(1)} collective-permute-done((f32[3,3,22,3]{3,2,1,0:T(8,128)S(1)}, f32[3,3,22,3]{3,2,1,0:T(8,128)S(1)}, u32[]{:S(2)}, u32[]{:S(2)}) %collective-permute-start.3) | collective-permute-done | bytes 2408 | tf_op jit(solution)/shard_map/ppermute | solution.py:29
  30.0 1.1 pad_maximum_fusion
  31.0 0.8 fusion.26
  32.2 0.7 fusion.22
  34.4 0.5 copy-done
  34.9 1.9 %fusion.14 = f32[256,9,3,16]{0,3,2,1:T(8,128)} fusion(f32[9,3,16,128]{3,2,1,0:T(8,128)S(1)} %constant_dynamic-update-slice_fusion, f32[256]{0:T(256)S(1)} %compare_select_fusion.4, s32[256]{0:T(256)S(1)} %add_select_fusion.4, s32[128]{0:T(128)S(1)} %iota_add_fusion, pred[256]{0:T(512)(128)(4,1)S(1)} %iota_compare_fusion), kind=kOutput, calls=%fused_computation.28 | convolution fusion | flops 170393600 | bytes 666368 | tf_op jit(solution)/shard_map/fpzx,xm->mfpz/dot_general | solution.py:159
  36.8 2.0 %reshape.198 = f32[16,16,9,3,16]{1,0,4,3,2:T(8,128)S(1)} reshape(f32[256,9,3,16]{0,3,2,1:T(8,128)} %fusion.14) | data formatting | bytes 884736 | tf_op jit(solution)/shard_map/reshape | solution.py:38
  38.8 2.8 %copy.45 = f32[16,16,9,3,16]{1,4,3,2,0:T(8,128)} copy(f32[16,16,9,3,16]{1,0,4,3,2:T(8,128)S(1)} %reshape.198) | data formatting | bytes 884736 | tf_op jit(solution)/shard_map/reshape | solution.py:38
  41.7 3.6 %reshape.222 = f32[16,1,6912]{2,1,0:T(1,128)} reshape(f32[16,9,3,16,16]{4,3,2,1,0:T(8,128)} %bitcast.73) | data formatting | bytes 884736
  45.3 7.4 %all-to-all-start = ((f32[16,1,6912]{2,1,0:T(1,128)}), f32[16,1,6912]{2,1,0:T(1,128)S(1)}, u32[]{:S(2)}, u32[]{:S(2)}) async-start(f32[16,1,6912]{2,1,0:T(1,128)} %reshape.222), calls=%async_computation | async-start | bytes 884736 | tf_op jit(solution)/shard_map/all_to_all | solution.py:44
  52.7 0.6 iota_add_fusion.1
  53.3 0.6 gather_fusion
  53.9 1.3 gather_fusion.1
  55.2 0.6 fusion.75
  56.3 0.5 slice_bitcast_fusion.1
  56.8 11.5 %all-to-all-done = f32[16,1,6912]{2,1,0:T(1,128)S(1)} async-done(((f32[16,1,6912]{2,1,0:T(1,128)}), f32[16,1,6912]{2,1,0:T(1,128)S(1)}, u32[]{:S(2)}, u32[]{:S(2)}) %all-to-all-start) | async-done | bytes 442400 | tf_op jit(solution)/shard_map/all_to_all | solution.py:44
  68.2 0.6 broadcast.354
  68.8 2.6 %reduce = f32[16,6912]{1,0:T(8,128)} reduce(f32[16,1,6912]{2,1,0:T(1,128)S(1)} %all-to-all-done, f32[]{:T(128)} %broadcast.354), dimensions={1}, to_apply=%all_to_all.12.reduce_sub_computation | reduce | bytes 884740 | tf_op jit(solution)/shard_map/all_to_all | solution.py:44
  71.4 2.2 %reshape.223 = f32[16,9,3,16,16]{4,3,2,1,0:T(8,128)S(1)} reshape(f32[16,6912]{1,0:T(8,128)} %reduce) | data formatting | bytes 884736
  74.3 3.1 %fusion.7 = f32[32,8,16,9,3]{0,2,4,3,1:T(8,128)} fusion(f32[16,9,3,16]{0,3,2,1:T(8,128)S(1)} %bitcast_reduce_fusion.1, f32[32,8]{0,1:T(8,128)S(1)} %fusion.76, s32[32,8]{0,1:T(8,128)S(1)} %add_select_fusion.3, s32[16]{0:T(128)S(1)} %copy-done.6, pred[32,8]{0,1:T(8,128)(4,1)S(1)} %copy-done.8), kind=kOutput, calls=%fused_computation.16 | convolution fusion | flops 21299200 | bytes 472384 | tf_op jit(solution)/shard_map/mfpz,zn->nmfp/dot_general | solution.py:163
  77.3 2.7 %copy.22 = f32[32,8,16,9,3]{2,1,4,3,0:T(8,128)S(1)} copy(f32[32,8,16,9,3]{0,2,4,3,1:T(8,128)} %fusion.7) | data formatting | bytes 884736 | tf_op jit(solution)/shard_map/mfpz,zn->nmfp/dot_general | solution.py:163
  80.0 2.0 %reshape.224 = f32[32,1,3456]{2,1,0:T(1,128)} reshape(f32[32,9,3,8,16]{4,3,2,1,0:T(8,128)S(1)} %bitcast.75) | data formatting | bytes 884736
  82.1 7.0 %all-to-all-start.1 = ((f32[32,1,3456]{2,1,0:T(1,128)}), f32[32,1,3456]{2,1,0:T(1,128)S(1)}, u32[]{:S(2)}, u32[]{:S(2)}) async-start(f32[32,1,3456]{2,1,0:T(1,128)} %reshape.224), calls=%async_computation.1 | async-start | bytes 884736 | tf_op jit(solution)/shard_map/all_to_all | solution.py:44
  89.1 0.7 and_select_fusion
  89.9 0.7 and_convert_fusion
  90.6 14.6 %all-to-all-done.1 = f32[32,1,3456]{2,1,0:T(1,128)S(1)} async-done(((f32[32,1,3456]{2,1,0:T(1,128)}), f32[32,1,3456]{2,1,0:T(1,128)S(1)}, u32[]{:S(2)}, u32[]{:S(2)}) %all-to-all-start.1) | async-done | bytes 442400 | tf_op jit(solution)/shard_map/all_to_all | solution.py:44
  105.2 2.6 %reduce.1 = f32[32,3456]{1,0:T(8,128)} reduce(f32[32,1,3456]{2,1,0:T(1,128)S(1)} %all-to-all-done.1, f32[]{:T(128)} %broadcast.354), dimensions={1}, to_apply=%all_to_all.13.reduce_sub_computation | reduce | bytes 884740 | tf_op jit(solution)/shard_map/all_to_all | solution.py:44
  107.7 2.2 %reshape.225 = f32[32,9,3,8,16]{4,3,2,1,0:T(8,128)S(1)} reshape(f32[32,3456]{1,0:T(8,128)} %reduce.1) | data formatting | bytes 884736
  110.9 2.0 %reshape.226 = f32[32,1,3456]{2,1,0:T(1,128)} reshape(f32[32,9,3,8,16]{4,3,2,1,0:T(8,128)S(1)} %broadcast_bitcast_fusion.1) | data formatting | bytes 884736
  113.0 18.6 %all_to_all.20 = f32[32,1,3456]{2,1,0:T(1,128)S(1)} all-to-all(f32[32,1,3456]{2,1,0:T(1,128)} %reshape.226), channel_id=1, replica_groups=mesh['gx'=16,'gz'=16,'grp'=2] {'gz','grp'}, dimensions={0} | all-to-all | bytes 884736 | tf_op jit(solution)/shard_map/all_to_all | solution.py:50
  131.6 2.6 %reduce.2 = f32[32,3456]{1,0:T(8,128)} reduce(f32[32,1,3456]{2,1,0:T(1,128)S(1)} %all_to_all.20, f32[]{:T(128)} %broadcast.354), dimensions={1}, to_apply=%all_to_all.14.reduce_sub_computation | reduce | bytes 884740 | tf_op jit(solution)/shard_map/all_to_all | solution.py:50
  134.2 2.2 %reshape.227 = f32[32,9,3,8,16]{4,3,2,1,0:T(8,128)S(1)} reshape(f32[32,3456]{1,0:T(8,128)} %reduce.2) | data formatting | bytes 884736
  136.4 2.1 %fusion = f32[16,9,3,16]{0,3,2,1:T(8,128)S(1)} fusion(s32[256]{0:T(256)S(1)} %add_select_fusion.4, s32[16]{0:T(128)S(1)} %copy-done.7, pred[256]{0:T(512)(128)(4,1)S(1)} %copy-done.11, f32[32,9,3,8,16]{4,3,2,1,0:T(8,128)S(1)} %reshape.227), kind=kOutput, calls=%fused_computation.2 | convolution fusion | flops 21295104 | bytes 471360 | tf_op jit(solution)/shard_map/nmfp,zn->mfpz/dot_general | solution.py:175
  138.7 2.0 %reshape.228 = f32[16,1,6912]{2,1,0:T(1,128)} reshape(f32[16,9,3,16,16]{4,3,2,1,0:T(8,128)S(1)} %broadcast_bitcast_fusion) | data formatting | bytes 884736
  140.7 22.5 %all_to_all.21 = f32[16,1,6912]{2,1,0:T(1,128)S(1)} all-to-all(f32[16,1,6912]{2,1,0:T(1,128)} %reshape.228), channel_id=1, replica_groups=mesh['gx'=16,'gz'=16,'grp'=2] {'gx'}, dimensions={0} | all-to-all | bytes 884736 | tf_op jit(solution)/shard_map/all_to_all | solution.py:50
  163.2 2.6 %reduce.3 = f32[16,6912]{1,0:T(8,128)} reduce(f32[16,1,6912]{2,1,0:T(1,128)S(1)} %all_to_all.21, f32[]{:T(128)} %broadcast.354), dimensions={1}, to_apply=%all_to_all.15.reduce_sub_computation | reduce | bytes 884740 | tf_op jit(solution)/shard_map/all_to_all | solution.py:50
  165.8 2.2 %reshape.229 = f32[16,9,3,16,16]{4,3,2,1,0:T(8,128)S(1)} reshape(f32[16,6912]{1,0:T(8,128)} %reduce.3) | data formatting | bytes 884736
  168.0 3.1 %copy.28 = f32[16,16,9,3,16]{1,0,4,3,2:T(8,128)} copy(f32[16,16,9,3,16]{1,4,3,2,0:T(8,128)S(1)} %bitcast.74) | data formatting | bytes 884736 | tf_op jit(solution)/shard_map/all_to_all | solution.py:50
  171.1 3.0 %reshape.200 = f32[256,9,3,16]{0,3,2,1:T(8,128)S(1)} reshape(f32[16,16,9,3,16]{1,0,4,3,2:T(8,128)} %copy.28) | data formatting | bytes 884736 | tf_op jit(solution)/shard_map/reshape | solution.py:56
  174.1 1.1 fusion.12
  175.3 0.7 copy-done.5
  (76 shorter events, 4.3 us)
Async XLA Ops:
  0.6 32.4 %copy-start.3 = (f32[3]{0:T(128)S(1)}, f32[3]{0:T(128)}, u32[]{:S(2)}) copy-start(f32[3]{0:T(128)} %param.5) | copy-start | bytes 40
  0.6 32.9 %copy-start.4 = (f32[3]{0:T(128)S(1)}, f32[3]{0:T(128)}, u32[]{:S(2)}) copy-start(f32[3]{0:T(128)} %param.6) | copy-start | bytes 40
  1.5 15.7 %collective-permute-start = (f32[3,3,3,128]{3,2,1,0:T(4,128)S(1)}, f32[3,3,3,128]{3,2,1,0:T(4,128)S(1)}, u32[]{:S(2)}, u32[]{:S(2)}) collective-permute-start(f32[3,3,3,128]{3,2,1,0:T(4,128)S(1)} %get-tuple-element.12), channel_id=1, source_target_pairs={{0,1},{1,2},{2,3},{3,4},{4,5},{5,6},{6,7},{7,8},{8,9},{9,10},{10,1... | collective-permute-start | bytes 41480 | tf_op jit(solution)/shard_map/ppermute | solution.py:27
  12.9 8.7 %collective-permute-start.1 = (f32[3,3,3,128]{3,2,1,0:T(4,128)S(1)}, f32[3,3,3,128]{3,2,1,0:T(4,128)S(1)}, u32[]{:S(2)}, u32[]{:S(2)}) collective-permute-start(f32[3,3,3,128]{3,2,1,0:T(4,128)S(1)} %get-tuple-element.13), channel_id=1, source_target_pairs={{1,0},{2,1},{3,2},{4,3},{5,4},{6,5},{7,6},{8,7},{9,8},{10,9},{11,1... | collective-permute-start | bytes 41480 | tf_op jit(solution)/shard_map/ppermute | solution.py:29
  17.2 17.2 %copy-start.10 = (pred[256]{0:T(512)(128)(4,1)}, pred[256]{0:T(512)(128)(4,1)S(1)}, u32[]{:S(2)}) copy-start(pred[256]{0:T(512)(128)(4,1)S(1)} %iota_compare_fusion) | copy-start | bytes 772
  22.7 4.9 %collective-permute-start.2 = (f32[3,3,22,3]{3,2,1,0:T(8,128)S(1)}, f32[3,3,22,3]{3,2,1,0:T(8,128)S(1)}, u32[]{:S(2)}, u32[]{:S(2)}) collective-permute-start(f32[3,3,22,3]{3,2,1,0:T(8,128)S(1)} %get-tuple-element.10), channel_id=1, source_target_pairs={{0,32},{32,64},{64,96},{96,128},{128,160},{160,192},{192,224},{224... | collective-permute-start | bytes 7136 | tf_op jit(solution)/shard_map/ppermute | solution.py:27
  25.8 4.2 %collective-permute-start.3 = (f32[3,3,22,3]{3,2,1,0:T(8,128)S(1)}, f32[3,3,22,3]{3,2,1,0:T(8,128)S(1)}, u32[]{:S(2)}, u32[]{:S(2)}) collective-permute-start(f32[3,3,22,3]{3,2,1,0:T(8,128)S(1)} %get-tuple-element.11), channel_id=1, source_target_pairs={{32,0},{64,32},{96,64},{128,96},{160,128},{192,160},{224,192},{256... | collective-permute-start | bytes 7136 | tf_op jit(solution)/shard_map/ppermute | solution.py:29
  25.8 8.6 %copy-start.14 = (s32[128]{0:T(128)}, s32[128]{0:T(128)S(1)}, u32[]{:S(2)}) copy-start(s32[128]{0:T(128)S(1)} %iota_add_fusion) | copy-start | bytes 1540
  31.0 3.1 %copy-start.1 = (f32[3,3,16,128]{3,2,1,0:T(8,128)S(1)}, f32[3,3,16,128]{3,2,1,0:T(8,128)}, u32[]{:S(2)}) copy-start(f32[3,3,16,128]{3,2,1,0:T(8,128)} %param.4) | copy-start | bytes 221188
  34.3 0.6 copy-start
  41.7 14.6 %copy-start.9 = (s32[3,2]{0,1:T(2,128)S(1)}, s32[3,2]{0,1:T(2,128)}, u32[]{:S(2)}) copy-start(s32[3,2]{0,1:T(2,128)} %param.7) | copy-start | bytes 76
  45.3 22.9 %all-to-all-start = ((f32[16,1,6912]{2,1,0:T(1,128)}), f32[16,1,6912]{2,1,0:T(1,128)S(1)}, u32[]{:S(2)}, u32[]{:S(2)}) async-start(f32[16,1,6912]{2,1,0:T(1,128)} %reshape.222), calls=%async_computation | async-start | bytes 884736 | tf_op jit(solution)/shard_map/all_to_all | solution.py:44
  73.6 0.7 copy-start.6
  73.6 0.7 copy-start.8
  80.0 9.7 %copy-start.13 = (s32[3]{0:T(128)S(1)}, s32[3]{0:T(128)}, u32[]{:S(2)}) copy-start(s32[3]{0:T(128)} %get-tuple-element.15) | copy-start | bytes 40
  80.0 9.8 %copy-start.12 = (s32[8]{0:T(128)S(1)}, s32[8]{0:T(128)}, u32[]{:S(2)}) copy-start(s32[8]{0:T(128)} %and_select_fusion.1) | copy-start | bytes 100
  82.1 23.1 %all-to-all-start.1 = ((f32[32,1,3456]{2,1,0:T(1,128)}), f32[32,1,3456]{2,1,0:T(1,128)S(1)}, u32[]{:S(2)}, u32[]{:S(2)}) async-start(f32[32,1,3456]{2,1,0:T(1,128)} %reshape.224), calls=%async_computation.1 | async-start | bytes 884736 | tf_op jit(solution)/shard_map/all_to_all | solution.py:44
  109.9 0.7 copy-start.2
  113.0 23.4 %copy-start.7 = (s32[16]{0:T(128)S(1)}, s32[16]{0:T(128)}, u32[]{:S(2)}) copy-start(s32[16]{0:T(128)} %iota_add_fusion.1) | copy-start | bytes 196
  113.0 23.4 %copy-start.11 = (pred[256]{0:T(512)(128)(4,1)S(1)}, pred[256]{0:T(512)(128)(4,1)}, u32[]{:S(2)}) copy-start(pred[256]{0:T(512)(128)(4,1)} %copy-done.10) | copy-start | bytes 772
  171.1 3.0 %copy-start.15 = (s32[128]{0:T(128)S(1)}, s32[128]{0:T(128)}, u32[]{:S(2)}) copy-start(s32[128]{0:T(128)} %copy-done.14) | copy-start | bytes 1540
  175.3 0.7 copy-start.5
where the time goes:
time: 177 us; the launch traced here: 176 us
  blocking collectives  41.1 us (23%)
  local copies, waits for them, and re-layouts  38.6 us (22%)
  waiting for transfers between devices  34.7 us (20%)
  starting transfers between devices  33.1 us (19%)
  other arithmetic  19.2 us (11%)
  matrix products  8.13 us (5%)
    all_to_all x2, blocking collectives, copy_for_each(): return lax.all_to_all(copies, axis, split_axis=0, concat_axis=0, tiled=True)  41.1 us
    all_to_all x2, waiting for transfers between devices, summed_on_arrival(): tiles = lax.all_to_all(split_up(shard, dim, count), axis, 0, 0, tiled=True)  26 us
    unnamed x42, local copies, waits for them, and re-layouts  21 us
    ppermute x2, starting transfers between devices, with_halo(): lax.ppermute(tail, axis, [(i, (i + 1) % count) for i in range(count)])  14.6 us
    all_to_all x2, starting transfers between devices, summed_on_arrival(): tiles = lax.all_to_all(split_up(shard, dim, count), axis, 0, 0, tiled=True)  14.4 us
    ppermute x2, waiting for transfers between devices, with_halo(): lax.ppermute(head, axis, [((i + 1) % count, i) for i in range(count)])  6.9 us
    all_to_all x2, other arithmetic, copy_for_each(): return lax.all_to_all(copies, axis, split_axis=0, concat_axis=0, tiled=True)  5.15 us
    all_to_all x2, other arithmetic, summed_on_arrival(): tiles = lax.all_to_all(split_up(shard, dim, count), axis, 0, 0, tiled=True)  5.15 us
  transfers between devices with their start and end apart: 6, of which 5 were waited for; matrix products, arithmetic and copies ran while one was open for 3% of the time, Pallas kernels for 0%

commit v1 on v0

v1 whole, which is shorter than its diff:
```python
import math

import jax
import jax.numpy as jnp
import numpy as np
from jax import lax
from jax.experimental import pallas as pl
from jax.experimental.pallas import tpu as pltpu
from jax.sharding import PartitionSpec as P

NX = 2048
NZ = 512
MODES = 256
HALF = MODES // 2
PLANES = 3
TILE_Z = 16
TILE_X = 128
GX = NX // TILE_X
GZ = NZ // TILE_Z
LANES = 128

molecular_diffusivity = 0.4
time_step = 0.2
highest = lax.Precision.HIGHEST
spanwise = ("gz", "grp")
pair_first = (0, 0, 0, 1, 1, 2)
pair_second = (0, 1, 2, 1, 2, 2)


def roll(values, shift, axis):
    return pltpu.roll(values, shift % values.shape[axis], axis)


def call(body, out_shapes, smem, *args):
    count = len(args)

    def kernel(*refs):
        ins = list(refs[:smem]) + [ref[...] for ref in refs[smem:count]]
        for ref, value in zip(refs[count:], body(*ins)):
            ref[...] = value

    return pl.pallas_call(
        kernel,
        out_shape=[jax.ShapeDtypeStruct(shape, jnp.float32) for shape in out_shapes],
        in_specs=[pl.BlockSpec(memory_space=pltpu.SMEM)] * smem
        + [pl.BlockSpec(memory_space=pltpu.VMEM)] * (count - smem),
        out_specs=[pl.BlockSpec(memory_space=pltpu.VMEM)] * len(out_shapes),
    )(*args)


def dot(left, right, left_dim=1, right_dim=0):
    return lax.dot_general(
        left,
        right,
        (((left_dim,), (right_dim,)), ((), ())),
        precision=highest,
        preferred_element_type=jnp.float32,
    )


def rate(components, downflow, shear):
    rates = []
    for index, cells in enumerate(components):
        east = roll(cells, -1, 1)
        west = roll(cells, 1, 1)
        north = roll(cells, -1, 0)
        south = roll(cells, 1, 0)
        result = (
            -(downflow + components[0]) * ((east - west) * 0.5)
            - components[2] * ((north - south) * 0.5)
            + molecular_diffusivity * (east + west + north + south - 4.0 * cells)
        )
        if index == 0:
            result = result - shear * components[1]
        rates.append(result)
    return rates


def advance_body(downflow, shear, own, left, right, synth_x):
    lane = lax.broadcasted_iota(jnp.int32, (24, LANES), 1)
    stepped = [[None] * PLANES for _ in range(3)]
    for p in range(PLANES):
        start = [
            jnp.concatenate(
                [own[c, p], jnp.where(lane < LANES // 2, right[c, p], left[c, p])], axis=1
            )
            for c in range(3)
        ]
        slope = rate(start, downflow[p], shear[p])
        first = [v + time_step * r for v, r in zip(start, slope)]
        slope = rate(first, downflow[p], shear[p])
        second = [
            0.75 * v + 0.25 * (f + time_step * r) for v, f, r in zip(start, first, slope)
        ]
        slope = rate(second, downflow[p], shear[p])
        for c in range(3):
            last = start[c] * (1.0 / 3.0) + (2.0 / 3.0) * (second[c] + time_step * slope[c])
            stepped[c][p] = last[:TILE_Z, :TILE_X]
    fields = [stepped[c][p] for c in range(3) for p in range(PLANES)]
    for a, b in zip(pair_first, pair_second):
        fields += [stepped[a][p] * stepped[b][p] for p in range(PLANES)]
    sums = []
    for tile in range(3):
        rows = jnp.concatenate(fields[8 * tile : 8 * tile + 8], axis=0)
        sums.append(dot(synth_x, rows, 1, 1).reshape(GX, 16, LANES))
    blank = jnp.zeros((TILE_Z, TILE_X), jnp.float32)
    rows = jnp.concatenate((fields[24:] + [blank]) * 2, axis=0)
    rest = dot(synth_x, rows, 1, 1).reshape(GX, 2, 8, LANES)
    lane = lax.broadcasted_iota(jnp.int32, (GX, 8, LANES), 2)
    sums.append(jnp.where(lane < LANES // 2, rest[:, 0], rest[:, 1]))
    advanced = jnp.stack([jnp.stack(stepped[c]) for c in range(3)])
    return advanced, jnp.concatenate(sums, axis=1)


def total_body(tiles):
    total = tiles[0]
    for index in range(1, GX):
        total = total + tiles[index]
    rest = total[48:56]
    lane = lax.broadcasted_iota(jnp.int32, (16, LANES), 1)
    rest = jnp.concatenate([rest, roll(rest, LANES // 2, 1)], axis=0)
    rest = jnp.where(lane < LANES // 2, rest, 0.0)
    upper = jnp.concatenate([total[0:16], total[16:32]], axis=1)
    lower = jnp.concatenate([total[32:48], rest], axis=1)
    return (jnp.concatenate([upper, lower], axis=0),)


def spanwise_body(place, counts, lines, analysis_z, synth_z):
    width = 2 * LANES
    in_block = lax.broadcasted_iota(jnp.int32, (GZ, width), 1) % TILE_Z
    spread = jnp.concatenate(
        [jnp.where(in_block == row, lines, 0.0) for row in range(TILE_Z)], axis=0
    )
    partial_sum = dot(analysis_z, spread)
    group = lax.broadcasted_iota(jnp.int32, (width, width), 0) // TILE_Z
    other = lax.broadcasted_iota(jnp.int32, (width, width), 1) // TILE_Z
    coeffs = dot(partial_sum, jnp.where(group == other, 1.0, 0.0))
    mode_x = place[0]
    number_x = jnp.where(mode_x < HALF, mode_x, mode_x - HALF + 1)
    weight_x = jnp.where(mode_x == 0, 1.0 / NX, 2.0 / NX)
    mode_z = lax.broadcasted_iota(jnp.int32, (MODES, width), 0)
    number_z = jnp.where(mode_z < HALF, mode_z, mode_z - HALF + 1)
    lane = lax.broadcasted_iota(jnp.int32, (MODES, width), 1)
    plane = (lane // TILE_Z + place[1]) % PLANES
    limit = jnp.zeros((MODES, width), jnp.int32)
    for p in range(PLANES):
        kept = jnp.where(number_x <= counts[p, 0], counts[p, 1], -1)
        limit = jnp.where(plane == p, kept, limit)
    coeffs = jnp.where(number_z <= limit, coeffs * weight_x, 0.0)
    rows = dot(synth_z, coeffs)
    result = jnp.zeros((GZ, width), jnp.float32)
    for row in range(TILE_Z):
        result = jnp.where(in_block == row, rows[row * GZ : (row + 1) * GZ], result)
    return (result,)


def stress_body(coeffs, synth_x):
    halves = []
    for half in range(2):
        block = coeffs[:, 16 * half : 16 * half + 16].reshape(MODES, 2 * LANES)
        halves.append(dot(block, synth_x, 0, 0))

    def filtered(field, plane):
        index = field * PLANES + plane
        start = index % 16 * TILE_Z
        return halves[index // 16][start : start + TILE_Z]

    stresses = []
    for q, (a, b) in enumerate(zip(pair_first, pair_second)):
        stresses.append(
            jnp.stack(
                [
                    filtered(3 + q, p) - filtered(a, p) * filtered(b, p)
                    for p in range(PLANES)
                ]
            )
        )
    return (jnp.stack(stresses),)


def spanwise_tables():
    column = np.arange(MODES)
    numbers = np.where(column < HALF, column, column - HALF + 1)
    positions = (np.arange(GZ)[None, :] * TILE_Z + np.arange(TILE_Z)[:, None]).reshape(-1)
    angles = (positions[:, None] * numbers[None, :] % NZ) * (2.0 * math.pi / NZ)
    synth = np.where(column[None, :] < HALF, np.cos(angles), np.sin(angles))
    weights = np.where(column == 0, 1.0 / NZ, 2.0 / NZ)
    analysis = (synth * weights[None, :]).T
    return np.ascontiguousarray(analysis, np.float32), synth.astype(np.float32)


def streamwise_table(start):
    column = jnp.arange(MODES, dtype=jnp.int32)
    numbers = jnp.where(column < HALF, column, column - HALF + 1)
    positions = start + jnp.arange(TILE_X, dtype=jnp.int32)
    phase_int = numbers[:, None] * positions[None, :] % NX
    angles = phase_int.astype(jnp.float32) * jnp.float32(2.0 * math.pi / NX)
    return jnp.where(column[:, None] < HALF, jnp.cos(angles), jnp.sin(angles))


def neighbours(lower, upper, axis):
    count = lax.axis_size(axis)
    before = lax.ppermute(upper, axis, [(i, (i + 1) % count) for i in range(count)])
    after = lax.ppermute(lower, axis, [((i + 1) % count, i) for i in range(count)])
    return before, after


def local(velocity, downflow, shear, mode_counts):
    here_x = lax.axis_index("gx")
    here_z = lax.axis_index(spanwise)
    above, below = neighbours(velocity[:, :, :3], velocity[:, :, -3:], spanwise)
    gap = jnp.zeros((3, PLANES, 2, TILE_X), jnp.float32)
    own = jnp.concatenate([velocity, below, gap, above], axis=2)
    left, right = neighbours(own, own, "gx")
    synth_x = streamwise_table(here_x * TILE_X)
    analysis_z, synth_z = (jnp.asarray(table) for table in spanwise_tables())

    advanced, sums = call(
        advance_body,
        [(3, PLANES, TILE_Z, TILE_X), (GX, 56, LANES)],
        2,
        downflow,
        shear,
        own,
        left,
        right,
        synth_x,
    )
    sums = lax.all_to_all(sums, "gx", 0, 0, tiled=True)
    (lines,) = call(total_body, [(GZ, 2 * LANES)], 0, sums)
    lines = lax.all_to_all(lines, spanwise, 0, 0, tiled=True)
    place = jnp.stack([here_x * 16 + here_z % 16, here_z // 16 * 16])
    (lines,) = call(
        spanwise_body,
        [(GZ, 2 * LANES)],
        2,
        place,
        mode_counts,
        lines,
        analysis_z,
        synth_z,
    )
    lines = lax.all_to_all(lines, spanwise, 0, 0, tiled=True)
    coeffs = lax.all_gather(lines, "gx")
    (stress,) = call(stress_body, [(6, PLANES, TILE_Z, TILE_X)], 0, coeffs, synth_x)
    return advanced, stress


def solution(mesh):
    return jax.shard_map(
        local,
        mesh=mesh,
        in_specs=(P(None, None, ("gz", "grp"), "gx"), P(), P(), P()),
        out_specs=(P(None, None, ("gz", "grp"), "gx"), P(None, None, ("gz", "grp"), "gx")),
        check_vma=False,
    )
```

time: 177 us -> 112 us (0.63)
  local copies, waits for them, and re-layouts: 38.6 us -> 7.97 us
  other arithmetic: 19.2 us -> 1.94 us
  blocking collectives: 41.1 us -> 29 us
  Pallas kernels: 0 us -> 11 us
  matrix products: 8.13 us -> 0 us
  waiting for transfers between devices: 34.7 us -> 29.6 us
  starting transfers between devices: 33.1 us -> 31 us
    all_to_all x2 -> x1, blocking collectives: 41.1 us -> 11.7 us  [local(): lines = lax.all_to_all(lines, spanwise, 0, 0, tiled=True)]
    all_gather x0 -> x1, blocking collectives: none -> 17.3 us  [local(): coeffs = lax.all_gather(lines, 'gx')]
    unnamed x42 -> x15, local copies, waits for them, and re-layouts: 21 us -> 4.87 us
    pallas_call x0 -> x4, Pallas kernels: none -> 11 us  [call(): pl.pallas_call(kernel, out_shape=[jax.ShapeDtypeStruct(shape, jnp.float32...]
    all_to_all x4 -> x0, other arithmetic: 10.3 us -> none  [the longest x2 5.15 us: copy_for_each(): return lax.all_to_all(copies, axis, split_axis=0, concat_axis=0, tiled=True)]
    dot_general x4 -> x0, matrix products: 8.13 us -> none  [the longest x1 3.07 us: local(): jnp.einsum('mfpz,zn->nmfp', streamwise, columns, precision=highest)]
    reshape x3 -> x0, local copies, waits for them, and re-layouts: 7.84 us -> none  [the longest x2 4.88 us: split_up(): shard.reshape(*shape[:dim], count, shape[dim] // count, *shape[dim + 1:])]
    all_to_all x2, waiting for transfers between devices: 26 us -> 22.7 us  [the longest x1 14.5 us: local(): sums = lax.all_to_all(sums, 'gx', 0, 0, tiled=True)]
  transfers between devices with their start and end apart: 6 -> 6, of which waited for: 5 -> 4; matrix products, arithmetic and copies ran while one was open for 3% -> 2% of each run, Pallas kernels for 0% -> 0%
where the time goes in v1:
time: 112 us; the launch traced here: 111 us
  starting transfers between devices  31 us (28%)
  waiting for transfers between devices  29.6 us (26%)
  blocking collectives  29 us (26%)
  Pallas kernels  11 us (10%)
  local copies, waits for them, and re-layouts  7.97 us (7%)
  other arithmetic  1.94 us (2%)
    all_gather x1, blocking collectives, local(): coeffs = lax.all_gather(lines, 'gx')  17.3 us
    ppermute x2, starting transfers between devices, neighbours(): lax.ppermute(lower, axis, [((i + 1) % count, i) for i in range(count)])  15.8 us
    all_to_all x1, waiting for transfers between devices, local(): sums = lax.all_to_all(sums, 'gx', 0, 0, tiled=True)  14.5 us
    all_to_all x1, blocking collectives, local(): lines = lax.all_to_all(lines, spanwise, 0, 0, tiled=True)  11.7 us
    pallas_call x4, Pallas kernels, call(): pl.pallas_call(kernel, out_shape=[jax.ShapeDtypeStruct(shape, jnp.float32...  11 us
    all_to_all x1, starting transfers between devices, local(): sums = lax.all_to_all(sums, 'gx', 0, 0, tiled=True)  8.26 us
    all_to_all x1, waiting for transfers between devices, local(): lines = lax.all_to_all(lines, spanwise, 0, 0, tiled=True)  8.15 us
    ppermute x2, waiting for transfers between devices, neighbours(): lax.ppermute(upper, axis, [(i, (i + 1) % count) for i in range(count)])  5.77 us
  transfers between devices with their start and end apart: 6, of which 4 were waited for; matrix products, arithmetic and copies ran while one was open for 2% of the time, Pallas kernels for 0%

profile of v1, /device:TPU:1, one launch (start us, length us, event | category | flops | bytes accessed | tf_op | source)
XLA Modules:
  0.0 111.2 jit_solution(10641037168835349696)
XLA Ops:
  0.6 0.0 copy-start.2
  0.6 0.8 fusion.3
  1.5 13.7 %collective-permute-start = (f32[3,3,3,128]{3,2,1,0:T(4,128)S(1)}, f32[3,3,3,128]{3,2,1,0:T(4,128)S(1)}, u32[]{:S(2)}, u32[]{:S(2)}) collective-permute-start(f32[3,3,3,128]{3,2,1,0:T(4,128)S(1)} %get-tuple-element.6), channel_id=1, source_target_pairs={{1,0},{2,1},{3,2},{4,3},{5,4},{6,5},{7,6},{8,7},{9,8},{10,9},{11,1... | collective-permute-start | bytes 41480 | tf_op jit(solution)/shard_map/ppermute | solution.py:204
  15.2 1.9 %collective-permute-start.1 = (f32[3,3,3,128]{3,2,1,0:T(4,128)S(1)}, f32[3,3,3,128]{3,2,1,0:T(4,128)S(1)}, u32[]{:S(2)}, u32[]{:S(2)}) collective-permute-start(f32[3,3,3,128]{3,2,1,0:T(4,128)S(1)} %get-tuple-element.7), channel_id=1, source_target_pairs={{0,1},{1,2},{2,3},{3,4},{4,5},{5,6},{6,7},{7,8},{8,9},{9,10},{10,1... | collective-permute-start | bytes 41480 | tf_op jit(solution)/shard_map/ppermute | solution.py:203
  17.2 0.1 pad.4.clone
  17.2 0.0 collective-permute-done
  17.2 5.8 %collective-permute-done.1 = f32[3,3,3,128]{3,2,1,0:T(4,128)S(1)} collective-permute-done((f32[3,3,3,128]{3,2,1,0:T(4,128)S(1)}, f32[3,3,3,128]{3,2,1,0:T(4,128)S(1)}, u32[]{:S(2)}, u32[]{:S(2)}) %collective-permute-start.1) | collective-permute-done | bytes 13856 | tf_op jit(solution)/shard_map/ppermute | solution.py:203
  23.0 0.0 copy-done.2
  23.0 0.1 pad_maximum_fusion.refs_2_
  23.1 0.0 copy-start.1
  23.1 2.1 %collective-permute-start.3 = (f32[3,3,24,128]{3,2,1,0:T(8,128)S(1)}, f32[3,3,24,128]{3,2,1,0:T(8,128)S(1)}, u32[]{:S(2)}, u32[]{:S(2)}) collective-permute-start(f32[3,3,24,128]{3,2,1,0:T(8,128)S(1)} %pad_maximum_fusion.refs_2_), channel_id=1, source_target_pairs={{32,0},{64,32},{96,64},{128,96},{160,128},{192,160},{224,192},{256... | collective-permute-start | bytes 331784 | tf_op jit(solution)/shard_map/ppermute | solution.py:204
  25.2 1.2 %collective-permute-start.2 = (f32[3,3,24,128]{3,2,1,0:T(8,128)S(1)}, f32[3,3,24,128]{3,2,1,0:T(8,128)S(1)}, u32[]{:S(2)}, u32[]{:S(2)}) collective-permute-start(f32[3,3,24,128]{3,2,1,0:T(8,128)S(1)} %pad_maximum_fusion.refs_2_), channel_id=1, source_target_pairs={{0,32},{32,64},{64,96},{96,128},{128,160},{160,192},{192,224},{224... | collective-permute-start | bytes 331784 | tf_op jit(solution)/shard_map/ppermute | solution.py:203
  26.4 1.3 %sine_select_fusion.refs_5_.refs_1_ = f32[256,128]{1,0:T(8,128)} fusion(s32[128]{0:T(128)S(1)} %iota_add_fusion, s32[256]{0:T(256)S(1)} %add_select_fusion.1, pred[256]{0:T(512)(128)(4,1)S(1)} %iota_compare_fusion), kind=kLoop, calls=%fused_computation.8 | loop fusion | flops 491520 | bytes 132864 | tf_op jit(solution)/shard_map/jit(_where)/select_n | solution.py:198
  27.7 1.1 %collective-permute-done.3.refs_4_ = f32[3,3,24,128]{3,2,1,0:T(8,128)S(1)} collective-permute-done((f32[3,3,24,128]{3,2,1,0:T(8,128)S(1)}, f32[3,3,24,128]{3,2,1,0:T(8,128)S(1)}, u32[]{:S(2)}, u32[]{:S(2)}) %collective-permute-start.3) | collective-permute-done | bytes 110624 | tf_op jit(solution)/shard_map/ppermute | solution.py:204
  28.8 0.0 copy-start.3
  28.8 0.0 collective-permute-done.2.refs_3_
  28.8 0.0 copy-done.1
  28.8 0.6 copy-done.3
  29.5 0.0 copy-start.4
  29.5 0.6 copy-done.4
  30.1 2.9 %shard_map.77 = (f32[3,3,16,128]{3,2,1,0:T(8,128)}, f32[16,56,128]{2,1,0:T(8,128)}) custom-call(f32[3]{0:T(128)} %refs_0_.1, f32[3]{0:T(128)} %refs_1_.2, f32[3,3,24,128]{3,2,1,0:T(8,128)} %copy-done.1, f32[3,3,24,128]{3,2,1,0:T(8,128)} %copy-done.4, f32[3,3,24,128]{3,2,1,0:T(8,128)} %copy-done.3, f32[256,128]{1,0:T(8,128)} %sine_select_fusion.refs_5_.refs_1_), custom_call_target="tpu_custom_call" | custom-call | tf_op jit(solution)/shard_map/pallas_call | solution.py:42
  33.0 8.3 %all-to-all-start = ((f32[16,56,128]{2,1,0:T(8,128)}), f32[16,56,128]{2,1,0:T(8,128)S(1)}, u32[]{:S(2)}, u32[]{:S(2)}) async-start(f32[16,56,128]{2,1,0:T(8,128)} %get-tuple-element.5), calls=%async_computation | async-start | bytes 917504 | tf_op jit(solution)/shard_map/all_to_all | solution.py:229
  41.2 0.0 copy-start.5
  41.3 0.7 copy-done.5
  41.9 0.7 copy.13.refs_1_
  42.6 14.5 %all-to-all-done.refs_0_ = f32[16,56,128]{2,1,0:T(8,128)S(1)} async-done(((f32[16,56,128]{2,1,0:T(8,128)}), f32[16,56,128]{2,1,0:T(8,128)S(1)}, u32[]{:S(2)}, u32[]{:S(2)}) %all-to-all-start) | async-done | bytes 458784 | tf_op jit(solution)/shard_map/all_to_all | solution.py:229
  57.1 0.0 copy-start
  57.1 0.8 copy-done
  57.9 1.7 %shard_map.78 = f32[32,256]{1,0:T(8,128)} custom-call(f32[16,56,128]{2,1,0:T(8,128)} %copy-done), custom_call_target="tpu_custom_call" | custom-call | tf_op jit(solution)/shard_map/pallas_call | solution.py:42
  59.6 1.4 %copy.12 = f32[32,1,256]{2,1,0:T(1,128)} copy(f32[32,1,256]{2,0,1:T(8,128)} %bitcast.11) | data formatting | bytes 65536 | tf_op jit(solution)/shard_map/all_to_all | solution.py:231
  61.0 3.8 %all-to-all-start.1 = ((f32[32,1,256]{2,1,0:T(1,128)}), f32[32,1,256]{2,1,0:T(1,128)S(1)}, u32[]{:S(2)}, u32[]{:S(2)}) async-start(f32[32,1,256]{2,1,0:T(1,128)} %copy.12), calls=%async_computation.1 | async-start | bytes 65536 | tf_op jit(solution)/shard_map/all_to_all | solution.py:231
  64.9 0.6 pad_add_fusion.refs_0_
  65.4 8.2 %all-to-all-done.1 = f32[32,1,256]{2,1,0:T(1,128)S(1)} async-done(((f32[32,1,256]{2,1,0:T(1,128)}), f32[32,1,256]{2,1,0:T(1,128)S(1)}, u32[]{:S(2)}, u32[]{:S(2)}) %all-to-all-start.1) | async-done | bytes 32800 | tf_op jit(solution)/shard_map/all_to_all | solution.py:231
  73.6 0.6 copy.18
  74.2 4.0 %shard_map.79 = f32[32,256]{1,0:T(8,128)} custom-call(s32[2]{0:T(128)} %pad_add_fusion.refs_0_, s32[3,2]{1,0:T(4,128)} %copy.13.refs_1_, f32[32,256]{1,0:T(8,128)} %bitcast.9, f32[256,512]{1,0:T(8,128)} %constant.70.clone.refs_3_, f32[512,256]{1,0:T(8,128)} %constant.71.clone.refs_4_), custom_call_target="tpu_custom_call" | custom-call | tf_op jit(solution)/shard_map/pallas_call | solution.py:42
  78.3 0.8 copy.14
  79.1 11.7 %all_to_all.25 = f32[32,1,256]{2,1,0:T(1,128)S(1)} all-to-all(f32[32,1,256]{2,1,0:T(1,128)S(1)} %copy.14), channel_id=1, replica_groups=mesh['gx'=16,'gz'=16,'grp'=2] {'gz','grp'}, dimensions={0} | all-to-all | bytes 65536 | tf_op jit(solution)/shard_map/all_to_all | solution.py:243
  90.7 17.3 %all-gather = f32[512,1,256]{2,1,0:T(1,128)S(1)} all-gather(f32[32,1,256]{2,1,0:T(1,128)S(1)} %all_to_all.25), channel_id=2, replica_groups=mesh['gx'=16,'gz'=16,'grp'=2] {'gx'}, dimensions={0}, use_global_device_ids=true | all-gather | bytes 557056 | tf_op jit(solution)/shard_map/all_gather | solution.py:244
  108.0 0.8 copy.16
  108.9 2.4 %shard_map.80 = f32[6,3,16,128]{3,2,1,0:T(8,128)} custom-call(f32[16,32,256]{2,1,0:T(8,128)} %bitcast.8, f32[256,128]{1,0:T(8,128)} %sine_select_fusion.refs_5_.refs_1_), custom_call_target="tpu_custom_call" | custom-call | tf_op jit(solution)/shard_map/pallas_call | solution.py:42
  (4 shorter events, 0.0 us)
Async XLA Ops:
  0.6 22.4 %copy-start.2 = (f32[3,3,16,128]{3,2,1,0:T(8,128)S(1)}, f32[3,3,16,128]{3,2,1,0:T(8,128)}, u32[]{:S(2)}) copy-start(f32[3,3,16,128]{3,2,1,0:T(8,128)} %param.6) | copy-start | bytes 221188
  1.5 15.7 %collective-permute-start = (f32[3,3,3,128]{3,2,1,0:T(4,128)S(1)}, f32[3,3,3,128]{3,2,1,0:T(4,128)S(1)}, u32[]{:S(2)}, u32[]{:S(2)}) collective-permute-start(f32[3,3,3,128]{3,2,1,0:T(4,128)S(1)} %get-tuple-element.6), channel_id=1, source_target_pairs={{1,0},{2,1},{3,2},{4,3},{5,4},{6,5},{7,6},{8,7},{9,8},{10,9},{11,1... | collective-permute-start | bytes 41480 | tf_op jit(solution)/shard_map/ppermute | solution.py:204
  15.2 7.8 %collective-permute-start.1 = (f32[3,3,3,128]{3,2,1,0:T(4,128)S(1)}, f32[3,3,3,128]{3,2,1,0:T(4,128)S(1)}, u32[]{:S(2)}, u32[]{:S(2)}) collective-permute-start(f32[3,3,3,128]{3,2,1,0:T(4,128)S(1)} %get-tuple-element.7), channel_id=1, source_target_pairs={{0,1},{1,2},{2,3},{3,4},{4,5},{5,6},{6,7},{7,8},{8,9},{9,10},{10,1... | collective-permute-start | bytes 41480 | tf_op jit(solution)/shard_map/ppermute | solution.py:203
  23.1 5.8 %copy-start.1 = (f32[3,3,24,128]{3,2,1,0:T(8,128)}, f32[3,3,24,128]{3,2,1,0:T(8,128)S(1)}, u32[]{:S(2)}) copy-start(f32[3,3,24,128]{3,2,1,0:T(8,128)S(1)} %pad_maximum_fusion.refs_2_) | copy-start | bytes 331780
  23.1 5.7 %collective-permute-start.3 = (f32[3,3,24,128]{3,2,1,0:T(8,128)S(1)}, f32[3,3,24,128]{3,2,1,0:T(8,128)S(1)}, u32[]{:S(2)}, u32[]{:S(2)}) collective-permute-start(f32[3,3,24,128]{3,2,1,0:T(8,128)S(1)} %pad_maximum_fusion.refs_2_), channel_id=1, source_target_pairs={{32,0},{64,32},{96,64},{128,96},{160,128},{192,160},{224,192},{256... | collective-permute-start | bytes 331784 | tf_op jit(solution)/shard_map/ppermute | solution.py:204
  25.2 3.6 %collective-permute-start.2 = (f32[3,3,24,128]{3,2,1,0:T(8,128)S(1)}, f32[3,3,24,128]{3,2,1,0:T(8,128)S(1)}, u32[]{:S(2)}, u32[]{:S(2)}) collective-permute-start(f32[3,3,24,128]{3,2,1,0:T(8,128)S(1)} %pad_maximum_fusion.refs_2_), channel_id=1, source_target_pairs={{0,32},{32,64},{64,96},{96,128},{128,160},{160,192},{192,224},{224... | collective-permute-start | bytes 331784 | tf_op jit(solution)/shard_map/ppermute | solution.py:203
  28.8 0.7 copy-start.3
  29.5 0.6 copy-start.4
  33.0 24.1 %all-to-all-start = ((f32[16,56,128]{2,1,0:T(8,128)}), f32[16,56,128]{2,1,0:T(8,128)S(1)}, u32[]{:S(2)}, u32[]{:S(2)}) async-start(f32[16,56,128]{2,1,0:T(8,128)} %get-tuple-element.5), calls=%async_computation | async-start | bytes 917504 | tf_op jit(solution)/shard_map/all_to_all | solution.py:229
  41.2 0.7 copy-start.5
  57.1 0.8 copy-start
  61.0 12.6 %all-to-all-start.1 = ((f32[32,1,256]{2,1,0:T(1,128)}), f32[32,1,256]{2,1,0:T(1,128)S(1)}, u32[]{:S(2)}, u32[]{:S(2)}) async-start(f32[32,1,256]{2,1,0:T(1,128)} %copy.12), calls=%async_computation.1 | async-start | bytes 65536 | tf_op jit(solution)/shard_map/all_to_all | solution.py:231

commit v2 on v0

v2 whole, which is shorter than its diff:
```python
import math

import jax
import jax.numpy as jnp
import numpy as np
from jax import lax
from jax.experimental import pallas as pl
from jax.experimental.pallas import tpu as pltpu
from jax.sharding import PartitionSpec as P

NX = 2048
NZ = 512
MODES = 256
HALF = MODES // 2
PLANES = 3
TILE_Z = 16
TILE_X = 128
GX = NX // TILE_X
GZ = NZ // TILE_Z
LANES = 128

SLOT = 14
STRIDE = PLANES * SLOT

molecular_diffusivity = 0.4
time_step = 0.2
highest = lax.Precision.HIGHEST
spanwise = ("gz", "grp")
pair_first = (0, 0, 0, 1, 1, 2)
pair_second = (0, 1, 2, 1, 2, 2)


def roll(values, shift, axis):
    shift = shift % values.shape[axis]
    return pltpu.roll(values, shift, axis) if shift else values


def call(body, out_shapes, smem, scratch, *args):
    return pl.pallas_call(
        body,
        out_shape=[jax.ShapeDtypeStruct(shape, jnp.float32) for shape in out_shapes],
        in_specs=[pl.BlockSpec(memory_space=pltpu.SMEM)] * smem
        + [pl.BlockSpec(memory_space=pltpu.VMEM)] * (len(args) - smem),
        out_specs=[pl.BlockSpec(memory_space=pltpu.VMEM)] * len(out_shapes),
        scratch_shapes=[pltpu.VMEM(shape, jnp.float32) for shape in scratch],
    )(*args)


def dot(left, right):
    return lax.dot_general(
        left,
        right,
        (((1,), (0,)), ((), ())),
        precision=highest,
        preferred_element_type=jnp.float32,
    )


def lanes_of(rows):
    return lax.broadcasted_iota(jnp.int32, (rows, LANES), 1)


def pack_body(own, left, right, out):
    lane = lanes_of(TILE_Z)
    cells = [own[c, p] for c in range(3) for p in range(PLANES)]
    for dest in range(GZ):
        if dest == 0:
            sides = [
                jnp.where(lane < LANES // 2, own[c, p], left[c, p])
                for c in range(3)
                for p in range(PLANES)
            ]
        elif dest == GZ - 1:
            sides = [
                jnp.where(lane < LANES // 2, right[c, p], own[c, p])
                for c in range(3)
                for p in range(PLANES)
            ]
        else:
            sides = cells
        packed = jnp.zeros((TILE_Z, LANES), jnp.float32)
        for index, values in enumerate(sides):
            moved = roll(values, index * SLOT - (4 * dest - 3), 1)
            here = (lane >= index * SLOT) & (lane < index * SLOT + 10)
            packed = jnp.where(here, moved, packed)
        out[dest] = packed


def advance_body(
    downflow, shear, counts, cells, table, sort_fields, sort_cells,
    out, start, first, second,
):
    chunk = 64
    edge = 8
    lane = lanes_of(chunk)
    component = lane // STRIDE
    plane = lane % STRIDE // SLOT
    flow = jnp.zeros((chunk, LANES), jnp.float32)
    slope = jnp.zeros((chunk, LANES), jnp.float32)
    for p in range(PLANES):
        flow = jnp.where(plane == p, downflow[p], flow)
        slope = jnp.where((plane == p) & (component == 0), shear[p], slope)

    def store(ref, row, values):
        ref[edge + row : edge + row + chunk] = values
        if row == 0:
            ref[edge + NZ : edge + NZ + edge] = values[:edge]
        if row == NZ - chunk:
            ref[:edge] = values[chunk - edge :]

    def rate(ref, row):
        low = edge + row
        middle = ref[low : low + chunk]
        north = ref[low + 1 : low + 1 + chunk]
        south = ref[low - 1 : low - 1 + chunk]
        east = roll(middle, -1, 1)
        west = roll(middle, 1, 1)
        next_one = roll(middle, -STRIDE, 1)
        along = jnp.where(
            component == 0,
            middle,
            jnp.where(component == 1, roll(middle, STRIDE, 1), roll(middle, 2 * STRIDE, 1)),
        )
        across = jnp.where(
            component == 2,
            middle,
            jnp.where(component == 1, next_one, roll(middle, -2 * STRIDE, 1)),
        )
        return middle, (
            -(flow + along) * ((east - west) * 0.5)
            - across * ((north - south) * 0.5)
            + molecular_diffusivity * (east + west + north + south - 4.0 * middle)
            - slope * next_one
        )

    rows = range(0, NZ, chunk)
    for row in rows:
        store(start, row, cells[row // 16 : (row + chunk) // 16].reshape(chunk, LANES))
    for row in rows:
        middle, change = rate(start, row)
        store(first, row, middle + time_step * change)
    for row in rows:
        middle, change = rate(first, row)
        begin = start[edge + row : edge + row + chunk]
        store(second, row, 0.75 * begin + 0.25 * (middle + time_step * change))
    part = (lane + LANES - 3) % LANES % SLOT // 4
    part = jnp.where((lane >= 3) & (lane < 127), part, 3)
    for row in rows:
        middle, change = rate(second, row)
        begin = start[edge + row : edge + row + chunk]
        last = begin * (1.0 / 3.0) + (2.0 / 3.0) * (middle + time_step * change)
        other = jnp.where(component == 2, roll(last, 2 * STRIDE, 1), roll(last, -STRIDE, 1))
        fields = jnp.where(part == 0, last, 0.0)
        fields = jnp.where(part == 1, roll(last * last, 4, 1), fields)
        first[row : row + chunk] = jnp.where(part == 2, roll(last * other, 8, 1), fields)
        sorted_cells = dot(jnp.where(part == 0, last, 0.0), sort_cells[...])
        sorted_cells = sorted_cells.reshape(chunk // 16, 2, 8, LANES)
        side = lax.broadcasted_iota(jnp.int32, (chunk // 16, 8, LANES), 2)
        out[row // 16 : (row + chunk) // 16, 16:24] = jnp.where(
            side < LANES // 2, sorted_cells[:, 0], sorted_cells[:, 1]
        )
    coeffs = dot(dot(table[...], first[:NZ]), sort_fields[...])
    mode = lax.broadcasted_iota(jnp.int32, (MODES, LANES), 0)
    number = jnp.where(mode < HALF, mode, mode - HALF + 1)
    plane = lanes_of(MODES) % 32 % PLANES
    limit = jnp.zeros((MODES, LANES), jnp.int32)
    for p in range(PLANES):
        limit = jnp.where(plane == p, counts[p, 1], limit)
    weight = jnp.where(mode == 0, 1.0 / NZ, 2.0 / NZ)
    coeffs = jnp.where(number <= limit, coeffs * weight, 0.0)
    out[:, 0:16] = dot(table[...].T, coeffs).reshape(GZ, 16, LANES)


def forward_body(cells, out):
    for row in range(TILE_Z):
        out[row] = cells[:, row, :]


def unsort():
    source = lax.broadcasted_iota(jnp.int32, (LANES, LANES), 0)
    target = lax.broadcasted_iota(jnp.int32, (LANES, LANES), 1)
    return jnp.where(target == source % 32 * 4 + source // 32, 1.0, 0.0)


def cells_body(cells, out, rows):
    lane = lanes_of(16)
    order = unsort()
    for group in range(2):
        stacked = jnp.concatenate(
            [cells[:, 16 + 4 * group + r, :] for r in range(4)], axis=0
        )
        turned = stacked.T
        for half in range(2):
            for r in range(4):
                joined = jnp.zeros((16, LANES), jnp.float32)
                for column in range(4):
                    begin = half * 64 + column * 16
                    moved = roll(turned[begin : begin + 16], (column - r) * 32, 1)
                    joined = jnp.where(lane // 32 == column, moved, joined)
                place = (half * 8 + group * 4 + r) * 16
                rows[place : place + 16] = joined
    rows[...] = dot(rows[...], order)
    for c in range(3):
        for p in range(PLANES):
            out[c, p] = rows[pl.ds(c * PLANES + p, TILE_Z, stride=16), :]


def streamwise_body(counts, lines, table, out, rows):
    cells = lines[...].reshape(NX // 4, LANES)
    coeffs = dot(table[0], cells)
    for column in range(1, 4):
        coeffs = coeffs + roll(dot(table[column], cells), -32 * column, 1)
    mode = lax.broadcasted_iota(jnp.int32, (MODES, LANES), 0)
    number = jnp.where(mode < HALF, mode, mode - HALF + 1)
    weight = jnp.where(mode == 0, 1.0 / NX, 2.0 / NX)
    lane = lanes_of(MODES)
    limit = jnp.full((MODES, LANES), -1, jnp.int32)
    for p in range(PLANES):
        limit = jnp.where((lane < 27) & (lane % PLANES == p), counts[p, 0], limit)
    coeffs = jnp.where(number <= limit, coeffs * weight, 0.0).T[:32]
    rows[...] = jnp.zeros(rows.shape, jnp.float32)
    for column in range(4):
        filtered = dot(coeffs, table[column])
        for q, (a, b) in enumerate(zip(pair_first, pair_second)):
            rows[column, 3 * q : 3 * q + 3] = (
                filtered[9 + 3 * q : 12 + 3 * q]
                - filtered[3 * a : 3 * a + 3] * filtered[3 * b : 3 * b + 3]
            )
    lane = lanes_of(24)
    for dest in range(GX):
        begin = dest // 4 * LANES
        joined = jnp.zeros((24, LANES), jnp.float32)
        for column in range(4):
            moved = roll(rows[column, :, begin : begin + LANES], (column - dest % 4) * 32, 1)
            joined = jnp.where(lane // 32 == column, moved, joined)
        out[dest] = joined


def stress_body(lines, out, rows):
    rows[...] = dot(lines[...].reshape(16 * 24, LANES), unsort())
    for q in range(6):
        for p in range(PLANES):
            out[q, p] = rows[pl.ds(q * PLANES + p, TILE_Z, stride=24), :]


def wave_table(length):
    column = np.arange(MODES)
    numbers = np.where(column < HALF, column, column - HALF + 1)
    angles = (np.arange(length)[:, None] * numbers[None, :] % length) * (2.0 * math.pi / length)
    return np.where(column[None, :] < HALF, np.cos(angles), np.sin(angles))


def tables():
    synth_z = wave_table(NZ).T
    synth_x = wave_table(NX).reshape(NX // 4, 4, MODES).transpose(1, 2, 0)
    sort_fields = np.zeros((LANES, LANES))
    sort_cells = np.zeros((LANES, LANES))
    kinds = ((0, 1, 2), (3, 6, 8), (4, 7, 5))
    for c in range(3):
        for p in range(PLANES):
            for column in range(4):
                lane = c * STRIDE + p * SLOT + 3 + column
                for kind in range(3):
                    field = kinds[kind][c] * PLANES + p
                    sort_fields[lane + 4 * kind, column * 32 + field] = 1.0
                for half in range(2):
                    sort_cells[lane, half * 64 + column * 16 + c * PLANES + p] = 1.0
    return [
        jnp.asarray(np.ascontiguousarray(values, dtype=np.float32))
        for values in (synth_z, sort_fields, sort_cells, synth_x)
    ]


def local(velocity, downflow, shear, mode_counts):
    count = lax.axis_size("gx")
    left = lax.ppermute(velocity, "gx", [(i, (i + 1) % count) for i in range(count)])
    right = lax.ppermute(velocity, "gx", [((i + 1) % count, i) for i in range(count)])
    synth_z, sort_fields, sort_cells, synth_x = tables()
    (cells,) = call(pack_body, [(GZ, TILE_Z, LANES)], 0, [], velocity, left, right)
    cells = lax.all_to_all(cells, spanwise, 0, 0, tiled=True)
    (cells,) = call(
        advance_body,
        [(GZ, 24, LANES)],
        3,
        [(NZ + 16, LANES)] * 3,
        downflow,
        shear,
        mode_counts,
        cells,
        synth_z,
        sort_fields,
        sort_cells,
    )
    cells = lax.all_to_all(cells, spanwise, 0, 0, tiled=True)
    (lines,) = call(forward_body, [(GX, GZ, LANES)], 0, [], cells)
    lines = lax.all_to_all(lines, "gx", 0, 0, tiled=True)
    (advanced,) = call(
        cells_body, [(3, PLANES, TILE_Z, TILE_X)], 0, [(16 * TILE_Z, LANES)], cells
    )
    (lines,) = call(
        streamwise_body,
        [(GX, 24, LANES)],
        1,
        [(4, 24, NX // 4)],
        mode_counts,
        lines,
        synth_x,
    )
    lines = lax.all_to_all(lines, "gx", 0, 0, tiled=True)
    (stress,) = call(
        stress_body, [(6, PLANES, TILE_Z, TILE_X)], 0, [(16 * 24, LANES)], lines
    )
    return advanced, stress


def solution(mesh):
    return jax.shard_map(
        local,
        mesh=mesh,
        in_specs=(P(None, None, ("gz", "grp"), "gx"), P(), P(), P()),
        out_specs=(P(None, None, ("gz", "grp"), "gx"), P(None, None, ("gz", "grp"), "gx")),
        check_vma=False,
    )
```

time: 177 us -> 104 us (0.59)
  local copies, waits for them, and re-layouts: 38.6 us -> 3.8 us
  Pallas kernels: 0 us -> 19.2 us
  other arithmetic: 19.2 us -> 0 us
  waiting for transfers between devices: 34.7 us -> 17.7 us
  starting transfers between devices: 33.1 us -> 21.4 us
  matrix products: 8.13 us -> 0 us
    pallas_call x0 -> x6, Pallas kernels: none -> 19.2 us  [call(): pl.pallas_call(body, out_shape=[jax.ShapeDtypeStruct(shape, jnp.float32)...]
    unnamed x42 -> x9, local copies, waits for them, and re-layouts: 21 us -> 3.8 us
    ppermute x4 -> x2, starting transfers between devices: 18.7 us -> 6.88 us  [the longest x1 4.19 us: local(): lax.ppermute(velocity, 'gx', [((i + 1) % count, i) for i in range(count)])]
    all_to_all x4 -> x0, other arithmetic: 10.3 us -> none  [the longest x2 5.15 us: copy_for_each(): return lax.all_to_all(copies, axis, split_axis=0, concat_axis=0, tiled=True)]
    all_to_all x2, waiting for transfers between devices: 26 us -> 16.6 us  [the longest x1 8.97 us: local(): cells = lax.all_to_all(cells, spanwise, 0, 0, tiled=True)]
    dot_general x4 -> x0, matrix products: 8.13 us -> none  [the longest x1 3.07 us: local(): jnp.einsum('mfpz,zn->nmfp', streamwise, columns, precision=highest)]
    reshape x3 -> x0, local copies, waits for them, and re-layouts: 7.84 us -> none  [the longest x2 4.88 us: split_up(): shard.reshape(*shape[:dim], count, shape[dim] // count, *shape[dim + 1:])]
    ppermute x4 -> x2, waiting for transfers between devices: 8.65 us -> 1.12 us  [the longest x1 0.95 us: local(): lax.ppermute(velocity, 'gx', [(i, (i + 1) % count) for i in range(count)])]
  transfers between devices with their start and end apart: 6 -> 4, of which waited for: 5 -> 4; matrix products, arithmetic and copies ran while one was open for 3% -> 1% of each run, Pallas kernels for 0% -> 2%
where the time goes in v2:
time: 104 us; the launch traced here: 103 us
  blocking collectives  40.7 us (39%)
  starting transfers between devices  21.4 us (21%)
  Pallas kernels  19.2 us (18%)
  waiting for transfers between devices  17.7 us (17%)
  local copies, waits for them, and re-layouts  3.8 us (4%)
    all_to_all x1, blocking collectives, local(): lines = lax.all_to_all(lines, 'gx', 0, 0, tiled=True)  22.2 us
    pallas_call x6, Pallas kernels, call(): pl.pallas_call(body, out_shape=[jax.ShapeDtypeStruct(shape, jnp.float32)...  19.2 us
    all_to_all x1, blocking collectives, local(): cells = lax.all_to_all(cells, spanwise, 0, 0, tiled=True)  18.4 us
    all_to_all x1, starting transfers between devices, local(): cells = lax.all_to_all(cells, spanwise, 0, 0, tiled=True)  11.1 us
    all_to_all x1, waiting for transfers between devices, local(): cells = lax.all_to_all(cells, spanwise, 0, 0, tiled=True)  8.97 us
    all_to_all x1, waiting for transfers between devices, local(): lines = lax.all_to_all(lines, 'gx', 0, 0, tiled=True)  7.63 us
    ppermute x1, starting transfers between devices, local(): lax.ppermute(velocity, 'gx', [((i + 1) % count, i) for i in range(count)])  4.19 us
    unnamed x9, local copies, waits for them, and re-layouts  3.8 us
  transfers between devices with their start and end apart: 4, of which 4 were waited for; matrix products, arithmetic and copies ran while one was open for 1% of the time, Pallas kernels for 2%

profile of v2, /device:TPU:1, one launch (start us, length us, event | category | flops | bytes accessed | tf_op | source)
XLA Modules:
  0.0 103.4 jit_solution(15003316129272974688)
XLA Ops:
  0.6 2.7 %collective-permute-start = (f32[3,3,16,128]{3,2,1,0:T(8,128)}, f32[3,3,16,128]{3,2,1,0:T(8,128)S(1)}, u32[]{:S(2)}, u32[]{:S(2)}) collective-permute-start(f32[3,3,16,128]{3,2,1,0:T(8,128)} %own.1), channel_id=1, source_target_pairs={{0,32},{32,64},{64,96},{96,128},{128,160},{160,192},{192,224},{224... | collective-permute-start | bytes 221192 | tf_op jit(solution)/shard_map/ppermute | solution.py:276
  3.3 4.2 %collective-permute-start.1 = (f32[3,3,16,128]{3,2,1,0:T(8,128)}, f32[3,3,16,128]{3,2,1,0:T(8,128)S(1)}, u32[]{:S(2)}, u32[]{:S(2)}) collective-permute-start(f32[3,3,16,128]{3,2,1,0:T(8,128)} %own.1), channel_id=1, source_target_pairs={{32,0},{64,32},{96,64},{128,96},{160,128},{192,160},{224,192},{256... | collective-permute-start | bytes 221192 | tf_op jit(solution)/shard_map/ppermute | solution.py:277
  7.5 0.9 collective-permute-done.left
  8.5 0.0 copy-start.2
  8.5 0.2 collective-permute-done.1.right
  8.6 0.5 copy-done.2
  9.1 0.0 copy-start.3
  9.1 0.6 copy-done.3
  9.7 2.3 %shard_map.95 = f32[32,16,128]{2,1,0:T(8,128)} custom-call(f32[3,3,16,128]{3,2,1,0:T(8,128)} %own.1, f32[3,3,16,128]{3,2,1,0:T(8,128)} %copy-done.2, f32[3,3,16,128]{3,2,1,0:T(8,128)} %copy-done.3), custom_call_target="tpu_custom_call" | custom-call | tf_op jit(solution)/shard_map/pallas_call | solution.py:39
  12.0 11.1 %all-to-all-start = ((f32[32,16,128]{2,1,0:T(8,128)}), f32[32,16,128]{2,1,0:T(8,128)S(1)}, u32[]{:S(2)}, u32[]{:S(2)}) async-start(f32[32,16,128]{2,1,0:T(8,128)} %shard_map.95), calls=%async_computation | async-start | bytes 524288 | tf_op jit(solution)/shard_map/all_to_all | solution.py:280
  23.2 1.3 %copy.10.counts = s32[3,2]{1,0:T(4,128)} copy(s32[3,2]{0,1:T(2,128)} %param.11) | data formatting | bytes 48 | tf_op args[3]
  24.5 9.0 %all-to-all-done.cells = f32[32,16,128]{2,1,0:T(8,128)S(1)} async-done(((f32[32,16,128]{2,1,0:T(8,128)}), f32[32,16,128]{2,1,0:T(8,128)S(1)}, u32[]{:S(2)}, u32[]{:S(2)}) %all-to-all-start) | async-done | bytes 262176 | tf_op jit(solution)/shard_map/all_to_all | solution.py:280
  33.5 0.0 copy-start
  33.5 0.7 copy-done
  34.2 5.3 %shard_map.96 = f32[32,24,128]{2,1,0:T(8,128)} custom-call(f32[3]{0:T(128)} %downflow.1, f32[3]{0:T(128)} %shear.1, s32[3,2]{1,0:T(4,128)} %copy.10.counts, f32[32,16,128]{2,1,0:T(8,128)} %copy-done, f32[256,512]{1,0:T(8,128)} %constant.8.clone.table, f32[128,128]{1,0:T(8,128)} %constant.9.clone.sort_fields, f32[128,128]{1,0:T(8,128)} %constant.10.clone.sort_cells), custom_call_target="tpu_custom_call" | custom-call | tf_op jit(solution)/shard_map/pallas_call | solution.py:39
  39.5 18.4 %all_to_all.20.cells = f32[32,24,128]{2,1,0:T(8,128)} all-to-all(f32[32,24,128]{2,1,0:T(8,128)} %shard_map.96), channel_id=1, replica_groups=mesh['gx'=16,'gz'=16,'grp'=2] {'gz','grp'}, dimensions={0} | all-to-all | bytes 786432 | tf_op jit(solution)/shard_map/all_to_all | solution.py:294
  57.9 1.8 %shard_map.98 = f32[16,32,128]{2,1,0:T(8,128)} custom-call(f32[32,24,128]{2,1,0:T(8,128)} %all_to_all.20.cells), custom_call_target="tpu_custom_call" | custom-call | tf_op jit(solution)/shard_map/pallas_call | solution.py:39
  59.8 22.2 %all_to_all.21.lines = f32[16,32,128]{2,1,0:T(8,128)} all-to-all(f32[16,32,128]{2,1,0:T(8,128)} %shard_map.98), channel_id=1, replica_groups=mesh['gx'=16,'gz'=16,'grp'=2] {'gx'}, dimensions={0} | all-to-all | bytes 524288 | tf_op jit(solution)/shard_map/all_to_all | solution.py:296
  82.0 5.6 %shard_map.99 = f32[16,24,128]{2,1,0:T(8,128)} custom-call(s32[3,2]{1,0:T(4,128)} %copy.10.counts, f32[16,32,128]{2,1,0:T(8,128)} %all_to_all.21.lines, f32[4,256,512]{2,1,0:T(8,128)} %constant.11.clone.table), custom_call_target="tpu_custom_call" | custom-call | tf_op jit(solution)/shard_map/pallas_call | solution.py:39
  87.6 3.4 %all-to-all-start.3 = ((f32[16,24,128]{2,1,0:T(8,128)}), f32[16,24,128]{2,1,0:T(8,128)S(1)}, u32[]{:S(2)}, u32[]{:S(2)}) async-start(f32[16,24,128]{2,1,0:T(8,128)} %shard_map.99), calls=%async_computation.3 | async-start | bytes 393216 | tf_op jit(solution)/shard_map/all_to_all | solution.py:309
  91.0 2.1 %shard_map.97 = f32[3,3,16,128]{3,2,1,0:T(8,128)} custom-call(f32[32,24,128]{2,1,0:T(8,128)} %all_to_all.20.cells), custom_call_target="tpu_custom_call" | custom-call | tf_op jit(solution)/shard_map/pallas_call | solution.py:39
  93.2 7.6 %all-to-all-done.3.lines = f32[16,24,128]{2,1,0:T(8,128)S(1)} async-done(((f32[16,24,128]{2,1,0:T(8,128)}), f32[16,24,128]{2,1,0:T(8,128)S(1)}, u32[]{:S(2)}, u32[]{:S(2)}) %all-to-all-start.3) | async-done | bytes 196640 | tf_op jit(solution)/shard_map/all_to_all | solution.py:309
  100.8 0.0 copy-start.1
  100.8 0.7 copy-done.1
  101.5 1.9 %shard_map.100 = f32[6,3,16,128]{3,2,1,0:T(8,128)} custom-call(f32[16,24,128]{2,1,0:T(8,128)} %copy-done.1), custom_call_target="tpu_custom_call" | custom-call | tf_op jit(solution)/shard_map/pallas_call | solution.py:39
Async XLA Ops:
  0.6 7.8 %collective-permute-start = (f32[3,3,16,128]{3,2,1,0:T(8,128)}, f32[3,3,16,128]{3,2,1,0:T(8,128)S(1)}, u32[]{:S(2)}, u32[]{:S(2)}) collective-permute-start(f32[3,3,16,128]{3,2,1,0:T(8,128)} %own.1), channel_id=1, source_target_pairs={{0,32},{32,64},{64,96},{96,128},{128,160},{160,192},{192,224},{224... | collective-permute-start | bytes 221192 | tf_op jit(solution)/shard_map/ppermute | solution.py:276
  3.3 5.3 %collective-permute-start.1 = (f32[3,3,16,128]{3,2,1,0:T(8,128)}, f32[3,3,16,128]{3,2,1,0:T(8,128)S(1)}, u32[]{:S(2)}, u32[]{:S(2)}) collective-permute-start(f32[3,3,16,128]{3,2,1,0:T(8,128)} %own.1), channel_id=1, source_target_pairs={{32,0},{64,32},{96,64},{128,96},{160,128},{192,160},{224,192},{256... | collective-permute-start | bytes 221192 | tf_op jit(solution)/shard_map/ppermute | solution.py:277
  8.5 0.6 copy-start.2
  9.1 0.6 copy-start.3
  12.0 21.4 %all-to-all-start = ((f32[32,16,128]{2,1,0:T(8,128)}), f32[32,16,128]{2,1,0:T(8,128)S(1)}, u32[]{:S(2)}, u32[]{:S(2)}) async-start(f32[32,16,128]{2,1,0:T(8,128)} %shard_map.95), calls=%async_computation | async-start | bytes 524288 | tf_op jit(solution)/shard_map/all_to_all | solution.py:280
  33.5 0.7 copy-start
  87.6 13.2 %all-to-all-start.3 = ((f32[16,24,128]{2,1,0:T(8,128)}), f32[16,24,128]{2,1,0:T(8,128)S(1)}, u32[]{:S(2)}, u32[]{:S(2)}) async-start(f32[16,24,128]{2,1,0:T(8,128)} %shard_map.99), calls=%async_computation.3 | async-start | bytes 393216 | tf_op jit(solution)/shard_map/all_to_all | solution.py:309
  100.8 0.7 copy-start.1

commit v3 on v2

--- a/solution.py
+++ b/solution.py
@@ -35,14 +35,26 @@
     return pltpu.roll(values, shift, axis) if shift else values
 
 
-def call(body, out_shapes, smem, scratch, *args):
+def call(body, out_shapes, smem, scratch, *args, tables=0, final=False, alias=None):
+    make = jax.ShapeDtypeStruct if final else pltpu.VMEM
+    near = len(args) - tables
+    args = (
+        args[:smem]
+        + tuple(pltpu.with_memory_space_constraint(arg, pltpu.VMEM) for arg in args[smem:near])
+        + args[near:]
+    )
+    fetched = [pltpu.VMEM(arg.shape, arg.dtype) for arg in args[near:]]
     return pl.pallas_call(
         body,
-        out_shape=[jax.ShapeDtypeStruct(shape, jnp.float32) for shape in out_shapes],
+        out_shape=[make(shape, jnp.float32) for shape in out_shapes],
         in_specs=[pl.BlockSpec(memory_space=pltpu.SMEM)] * smem
-        + [pl.BlockSpec(memory_space=pltpu.VMEM)] * (len(args) - smem),
+        + [pl.BlockSpec(memory_space=pltpu.VMEM)] * (near - smem)
+        + [pl.BlockSpec(memory_space=pl.ANY)] * tables,
         out_specs=[pl.BlockSpec(memory_space=pltpu.VMEM)] * len(out_shapes),
-        scratch_shapes=[pltpu.VMEM(shape, jnp.float32) for shape in scratch],
+        scratch_shapes=[pltpu.VMEM(shape, jnp.float32) for shape in scratch]
+        + fetched
+        + ([pltpu.SemaphoreType.DMA((4,))] if tables else []),
+        input_output_aliases=alias or {},
     )(*args)
 
 
@@ -60,36 +72,43 @@
     return lax.broadcasted_iota(jnp.int32, (rows, LANES), 1)
 
 
-def pack_body(own, left, right, out):
+def packed_for(dest, sides):
     lane = lanes_of(TILE_Z)
+    packed = jnp.zeros((TILE_Z, LANES), jnp.float32)
+    for index, values in enumerate(sides):
+        moved = roll(values, index * SLOT - (4 * dest - 3), 1)
+        here = (lane >= index * SLOT) & (lane < index * SLOT + 10)
+        packed = jnp.where(here, moved, packed)
+    return packed
+
+
+def inner_body(own, out):
     cells = [own[c, p] for c in range(3) for p in range(PLANES)]
-    for dest in range(GZ):
-        if dest == 0:
-            sides = [
-                jnp.where(lane < LANES // 2, own[c, p], left[c, p])
-                for c in range(3)
-                for p in range(PLANES)
-            ]
-        elif dest == GZ - 1:
-            sides = [
-                jnp.where(lane < LANES // 2, right[c, p], own[c, p])
-                for c in range(3)
-                for p in range(PLANES)
-            ]
-        else:
-            sides = cells
-        packed = jnp.zeros((TILE_Z, LANES), jnp.float32)
-        for index, values in enumerate(sides):
-            moved = roll(values, index * SLOT - (4 * dest - 3), 1)
-            here = (lane >= index * SLOT) & (lane < index * SLOT + 10)
-            packed = jnp.where(here, moved, packed)
-        out[dest] = packed
+    for dest in range(1, GZ - 1):
+        out[dest] = packed_for(dest, cells)
+    out[0] = packed_for(GZ // 2, cells)
+    out[GZ - 1] = packed_for(GZ // 2, cells)
+
+
+def outer_body(own, left, right, inner, out):
+    low = lanes_of(TILE_Z) < LANES // 2
+    pairs = [(c, p) for c in range(3) for p in range(PLANES)]
+    out[0] = packed_for(0, [jnp.where(low, own[c, p], left[c, p]) for c, p in pairs])
+    out[GZ - 1] = packed_for(
+        GZ - 1, [jnp.where(low, right[c, p], own[c, p]) for c, p in pairs]
+    )
 
 
 def advance_body(
-    downflow, shear, counts, cells, table, sort_fields, sort_cells,
-    out, start, first, second,
+    downflow, shear, counts, cells, far_table, far_fields, far_cells,
+    out, start, first, second, table, sort_fields, sort_cells, done,
 ):
+    fetch_table = pltpu.make_async_copy(far_table, table, done.at[0])
+    fetch_fields = pltpu.make_async_copy(far_fields, sort_fields, done.at[1])
+    fetch_cells = pltpu.make_async_copy(far_cells, sort_cells, done.at[2])
+    fetch_cells.start()
+    fetch_table.start()
+    fetch_fields.start()
     chunk = 64
     edge = 8
     lane = lanes_of(chunk)
@@ -143,6 +162,7 @@
         middle, change = rate(first, row)
         begin = start[edge + row : edge + row + chunk]
         store(second, row, 0.75 * begin + 0.25 * (middle + time_step * change))
+    fetch_cells.wait()
     part = (lane + LANES - 3) % LANES % SLOT // 4
     part = jnp.where((lane >= 3) & (lane < 127), part, 3)
     for row in rows:
@@ -159,13 +179,15 @@
         out[row // 16 : (row + chunk) // 16, 16:24] = jnp.where(
             side < LANES // 2, sorted_cells[:, 0], sorted_cells[:, 1]
         )
+    fetch_table.wait()
+    fetch_fields.wait()
     coeffs = dot(dot(table[...], first[:NZ]), sort_fields[...])
     mode = lax.broadcasted_iota(jnp.int32, (MODES, LANES), 0)
     number = jnp.where(mode < HALF, mode, mode - HALF + 1)
     plane = lanes_of(MODES) % 32 % PLANES
     limit = jnp.zeros((MODES, LANES), jnp.int32)
     for p in range(PLANES):
-        limit = jnp.where(plane == p, counts[p, 1], limit)
+        limit = jnp.where(plane == p, counts[1, p], limit)
     weight = jnp.where(mode == 0, 1.0 / NZ, 2.0 / NZ)
     coeffs = jnp.where(number <= limit, coeffs * weight, 0.0)
     out[:, 0:16] = dot(table[...].T, coeffs).reshape(GZ, 16, LANES)
@@ -205,10 +227,18 @@
             out[c, p] = rows[pl.ds(c * PLANES + p, TILE_Z, stride=16), :]
 
 
-def streamwise_body(counts, lines, table, out, rows):
+def streamwise_body(counts, lines, far_table, out, rows, table, done):
+    fetches = [
+        pltpu.make_async_copy(far_table.at[column], table.at[column], done.at[column])
+        for column in range(4)
+    ]
+    for fetch in fetches:
+        fetch.start()
     cells = lines[...].reshape(NX // 4, LANES)
+    fetches[0].wait()
     coeffs = dot(table[0], cells)
     for column in range(1, 4):
+        fetches[column].wait()
         coeffs = coeffs + roll(dot(table[column], cells), -32 * column, 1)
     mode = lax.broadcasted_iota(jnp.int32, (MODES, LANES), 0)
     number = jnp.where(mode < HALF, mode, mode - HALF + 1)
@@ -216,7 +246,7 @@
     lane = lanes_of(MODES)
     limit = jnp.full((MODES, LANES), -1, jnp.int32)
     for p in range(PLANES):
-        limit = jnp.where((lane < 27) & (lane % PLANES == p), counts[p, 0], limit)
+        limit = jnp.where((lane < 27) & (lane % PLANES == p), counts[0, p], limit)
     coeffs = jnp.where(number <= limit, coeffs * weight, 0.0).T[:32]
     rows[...] = jnp.zeros(rows.shape, jnp.float32)
     for column in range(4):
@@ -250,7 +280,7 @@
     return np.where(column[None, :] < HALF, np.cos(angles), np.sin(angles))
 
 
-def tables():
+def wave_tables():
     synth_z = wave_table(NZ).T
     synth_x = wave_table(NX).reshape(NX // 4, 4, MODES).transpose(1, 2, 0)
     sort_fields = np.zeros((LANES, LANES))
@@ -273,10 +303,22 @@
 
 def local(velocity, downflow, shear, mode_counts):
     count = lax.axis_size("gx")
+    mode_counts = mode_counts.T
     left = lax.ppermute(velocity, "gx", [(i, (i + 1) % count) for i in range(count)])
     right = lax.ppermute(velocity, "gx", [((i + 1) % count, i) for i in range(count)])
-    synth_z, sort_fields, sort_cells, synth_x = tables()
-    (cells,) = call(pack_body, [(GZ, TILE_Z, LANES)], 0, [], velocity, left, right)
+    synth_z, sort_fields, sort_cells, synth_x = wave_tables()
+    (inner,) = call(inner_body, [(GZ, TILE_Z, LANES)], 0, [], velocity)
+    (cells,) = call(
+        outer_body,
+        [(GZ, TILE_Z, LANES)],
+        0,
+        [],
+        velocity,
+        left,
+        right,
+        inner,
+        alias={3: 0},
+    )
     cells = lax.all_to_all(cells, spanwise, 0, 0, tiled=True)
     (cells,) = call(
         advance_body,
@@ -290,12 +332,13 @@
         synth_z,
         sort_fields,
         sort_cells,
+        tables=3,
     )
     cells = lax.all_to_all(cells, spanwise, 0, 0, tiled=True)
     (lines,) = call(forward_body, [(GX, GZ, LANES)], 0, [], cells)
     lines = lax.all_to_all(lines, "gx", 0, 0, tiled=True)
     (advanced,) = call(
-        cells_body, [(3, PLANES, TILE_Z, TILE_X)], 0, [(16 * TILE_Z, LANES)], cells
+        cells_body, [(3, PLANES, TILE_Z, TILE_X)], 0, [(16 * TILE_Z, LANES)], cells, final=True
     )
     (lines,) = call(
         streamwise_body,
@@ -305,10 +348,11 @@
         mode_counts,
         lines,
         synth_x,
+        tables=1,
     )
     lines = lax.all_to_all(lines, "gx", 0, 0, tiled=True)
     (stress,) = call(
-        stress_body, [(6, PLANES, TILE_Z, TILE_X)], 0, [(16 * 24, LANES)], lines
+        stress_body, [(6, PLANES, TILE_Z, TILE_X)], 0, [(16 * 24, LANES)], lines, final=True
     )
     return advanced, stress
 

time: 104 us -> 96.3 us (0.926)
  blocking collectives: 40.7 us -> 59.9 us
  starting transfers between devices: 21.4 us -> 10.3 us
  waiting for transfers between devices: 17.7 us -> 8.79 us
  Pallas kernels: 19.2 us -> 15.3 us
  local copies, waits for them, and re-layouts: 3.8 us -> 0.92 us
    all_to_all x1 -> x2, blocking collectives: 18.4 us -> 34.8 us  [local(): cells = lax.all_to_all(cells, spanwise, 0, 0, tiled=True)]
    all_to_all x1 -> x0, starting transfers between devices: 11.1 us -> none  [local(): cells = lax.all_to_all(cells, spanwise, 0, 0, tiled=True)]
    all_to_all x1 -> x0, waiting for transfers between devices: 8.97 us -> none  [local(): cells = lax.all_to_all(cells, spanwise, 0, 0, tiled=True)]
    pallas_call x6 -> x7, Pallas kernels: 19.2 us -> 15.3 us  [call(): pl.pallas_call(body, out_shape=[make(shape, jnp.float32) for shape in out...]
    all_to_all x1, blocking collectives: 22.2 us -> 25.2 us  [local(): lines = lax.all_to_all(lines, 'gx', 0, 0, tiled=True)]
    unnamed x9 -> x2, local copies, waits for them, and re-layouts: 3.8 us -> 0.92 us
    ppermute x1, starting transfers between devices: 2.69 us -> 0.01 us  [local(): lax.ppermute(velocity, 'gx', [(i, (i + 1) % count) for i in range(count)])]
    ppermute x1, starting transfers between devices: 4.19 us -> 6.85 us  [local(): lax.ppermute(velocity, 'gx', [((i + 1) % count, i) for i in range(count)])]
  transfers between devices with their start and end apart: 4 -> 3, of which waited for: 4 -> 2; matrix products, arithmetic and copies ran while one was open for 1% -> 0% of each run, Pallas kernels for 2% -> 2%
where the time goes in v3:
time: 96.3 us; the launch traced here: 95.9 us
  blocking collectives  59.9 us (62%)
  Pallas kernels  15.3 us (16%)
  starting transfers between devices  10.3 us (11%)
  waiting for transfers between devices  8.79 us (9%)
    all_to_all x2, blocking collectives, local(): cells = lax.all_to_all(cells, spanwise, 0, 0, tiled=True)  34.8 us
    all_to_all x1, blocking collectives, local(): lines = lax.all_to_all(lines, 'gx', 0, 0, tiled=True)  25.2 us
    pallas_call x7, Pallas kernels, call(): pl.pallas_call(body, out_shape=[make(shape, jnp.float32) for shape in out...  15.3 us
    all_to_all x1, waiting for transfers between devices, local(): lines = lax.all_to_all(lines, 'gx', 0, 0, tiled=True)  8.63 us
    ppermute x1, starting transfers between devices, local(): lax.ppermute(velocity, 'gx', [((i + 1) % count, i) for i in range(count)])  6.85 us
    all_to_all x1, starting transfers between devices, local(): lines = lax.all_to_all(lines, 'gx', 0, 0, tiled=True)  3.43 us
  transfers between devices with their start and end apart: 3, of which 2 were waited for; matrix products, arithmetic and copies ran while one was open for 0% of the time, Pallas kernels for 2%

profile of v3, /device:TPU:1, one launch (start us, length us, event | category | flops | bytes accessed | tf_op | source)
XLA Modules:
  0.0 95.9 jit_solution(459308617462645269)
XLA Ops:
  0.6 6.9 %collective-permute-start.1 = (f32[3,3,16,128]{3,2,1,0:T(8,128)}, f32[3,3,16,128]{3,2,1,0:T(8,128)S(1)}, u32[]{:S(2)}, u32[]{:S(2)}) collective-permute-start(f32[3,3,16,128]{3,2,1,0:T(8,128)} %own.3), channel_id=1, source_target_pairs={{32,0},{64,32},{96,64},{128,96},{160,128},{192,160},{224,192},{256... | collective-permute-start | bytes 221192 | tf_op jit(solution)/shard_map/ppermute | solution.py:308
  7.5 0.0 collective-permute-start
  7.5 0.0 copy-start
  7.5 0.9 copy-done
  8.4 0.6 shard_map.95.inner
  9.0 0.0 collective-permute-done.1.right
  9.0 0.2 collective-permute-done.left
  9.2 0.1 shard_map.96
  9.3 19.7 %all_to_all.20.cells = f32[32,16,128]{2,1,0:T(8,128)S(1)} all-to-all(f32[32,16,128]{2,1,0:T(8,128)S(1)} %shard_map.96), channel_id=1, replica_groups=mesh['gx'=16,'gz'=16,'grp'=2] {'gz','grp'}, dimensions={0} | all-to-all | bytes 524288 | tf_op jit(solution)/shard_map/all_to_all | solution.py:322
  29.0 5.2 %shard_map.97 = f32[32,24,128]{2,1,0:T(8,128)S(1)} custom-call(f32[3]{0:T(128)} %downflow.1, f32[3]{0:T(128)} %shear.1, s32[2,3]{1,0:T(2,128)} %bitcast.1, f32[32,16,128]{2,1,0:T(8,128)S(1)} %all_to_all.20.cells, f32[256,512]{1,0:T(8,128)} %constant.8.clone.far_table, f32[128,128]{1,0:T(8,128)} %constant.9.clone.far_fields, f32[128,128]{1,0:T(8,128)} %constant.10.clone.far_cells), custom_call_target="tpu_custom_call" | custom-call | tf_op jit(solution)/shard_map/pallas_call | solution.py:47
  34.2 15.1 %all_to_all.21.cells = f32[32,24,128]{2,1,0:T(8,128)S(1)} all-to-all(f32[32,24,128]{2,1,0:T(8,128)S(1)} %shard_map.97), channel_id=1, replica_groups=mesh['gx'=16,'gz'=16,'grp'=2] {'gz','grp'}, dimensions={0} | all-to-all | bytes 786432 | tf_op jit(solution)/shard_map/all_to_all | solution.py:337
  49.3 0.1 shard_map.99
  49.5 25.2 %all_to_all.22.lines = f32[16,32,128]{2,1,0:T(8,128)S(1)} all-to-all(f32[16,32,128]{2,1,0:T(8,128)S(1)} %shard_map.99), channel_id=1, replica_groups=mesh['gx'=16,'gz'=16,'grp'=2] {'gx'}, dimensions={0} | all-to-all | bytes 524288 | tf_op jit(solution)/shard_map/all_to_all | solution.py:339
  74.6 7.0 %shard_map.100 = f32[16,24,128]{2,1,0:T(8,128)} custom-call(s32[2,3]{1,0:T(2,128)} %bitcast.2, f32[16,32,128]{2,1,0:T(8,128)S(1)} %all_to_all.22.lines, f32[4,256,512]{2,1,0:T(8,128)} %constant.11.clone.far_table), custom_call_target="tpu_custom_call" | custom-call | tf_op jit(solution)/shard_map/pallas_call | solution.py:47
  81.7 3.4 %all-to-all-start.3 = ((f32[16,24,128]{2,1,0:T(8,128)}), f32[16,24,128]{2,1,0:T(8,128)S(1)}, u32[]{:S(2)}, u32[]{:S(2)}) async-start(f32[16,24,128]{2,1,0:T(8,128)} %shard_map.100), calls=%async_computation.3 | async-start | bytes 393216 | tf_op jit(solution)/shard_map/all_to_all | solution.py:353
  85.1 1.1 %shard_map.98 = f32[3,3,16,128]{3,2,1,0:T(8,128)} custom-call(f32[32,24,128]{2,1,0:T(8,128)S(1)} %all_to_all.21.cells), custom_call_target="tpu_custom_call" | custom-call | tf_op jit(solution)/shard_map/pallas_call | solution.py:47
  86.2 8.6 %all-to-all-done.3.lines = f32[16,24,128]{2,1,0:T(8,128)S(1)} async-done(((f32[16,24,128]{2,1,0:T(8,128)}), f32[16,24,128]{2,1,0:T(8,128)S(1)}, u32[]{:S(2)}, u32[]{:S(2)}) %all-to-all-start.3) | async-done | bytes 196640 | tf_op jit(solution)/shard_map/all_to_all | solution.py:353
  94.9 1.0 %shard_map.101 = f32[6,3,16,128]{3,2,1,0:T(8,128)} custom-call(f32[16,24,128]{2,1,0:T(8,128)S(1)} %all-to-all-done.3.lines), custom_call_target="tpu_custom_call" | custom-call | tf_op jit(solution)/shard_map/pallas_call | solution.py:47
Async XLA Ops:
  0.6 8.4 %collective-permute-start.1 = (f32[3,3,16,128]{3,2,1,0:T(8,128)}, f32[3,3,16,128]{3,2,1,0:T(8,128)S(1)}, u32[]{:S(2)}, u32[]{:S(2)}) collective-permute-start(f32[3,3,16,128]{3,2,1,0:T(8,128)} %own.3), channel_id=1, source_target_pairs={{32,0},{64,32},{96,64},{128,96},{160,128},{192,160},{224,192},{256... | collective-permute-start | bytes 221192 | tf_op jit(solution)/shard_map/ppermute | solution.py:308
  7.5 1.7 %collective-permute-start = (f32[3,3,16,128]{3,2,1,0:T(8,128)}, f32[3,3,16,128]{3,2,1,0:T(8,128)S(1)}, u32[]{:S(2)}, u32[]{:S(2)}) collective-permute-start(f32[3,3,16,128]{3,2,1,0:T(8,128)} %own.3), channel_id=1, source_target_pairs={{0,32},{32,64},{64,96},{96,128},{128,160},{160,192},{192,224},{224... | collective-permute-start | bytes 221192 | tf_op jit(solution)/shard_map/ppermute | solution.py:307
  7.5 0.9 copy-start
  81.7 13.2 %all-to-all-start.3 = ((f32[16,24,128]{2,1,0:T(8,128)}), f32[16,24,128]{2,1,0:T(8,128)S(1)}, u32[]{:S(2)}, u32[]{:S(2)}) async-start(f32[16,24,128]{2,1,0:T(8,128)} %shard_map.100), calls=%async_computation.3 | async-start | bytes 393216 | tf_op jit(solution)/shard_map/all_to_all | solution.py:353

commit v4 on v3

--- a/solution.py
+++ b/solution.py
@@ -24,7 +24,6 @@
 
 molecular_diffusivity = 0.4
 time_step = 0.2
-highest = lax.Precision.HIGHEST
 spanwise = ("gz", "grp")
 pair_first = (0, 0, 0, 1, 1, 2)
 pair_second = (0, 1, 2, 1, 2, 2)
@@ -63,9 +62,38 @@
         left,
         right,
         (((1,), (0,)), ((), ())),
-        precision=highest,
+        precision=lax.Precision.DEFAULT,
         preferred_element_type=jnp.float32,
     )
+
+
+def parts(values, count):
+    terms = []
+    for index in range(count):
+        terms.append(values.astype(jnp.bfloat16))
+        if index + 1 < count:
+            values = values - terms[-1].astype(jnp.float32)
+    return terms
+
+
+def picked(values, choice):
+    rows = values.shape[0]
+    sums = dot(jnp.concatenate(parts(values, 3), axis=0), choice)
+    return sums[:rows] + (sums[rows : 2 * rows] + sums[2 * rows :])
+
+
+def table_dot(high, low, values):
+    width = values.shape[1]
+    large, small = parts(values, 2)
+    sums = dot(high, jnp.concatenate([large, small], axis=1))
+    return sums[:, :width] + (sums[:, width:] + dot(low, large))
+
+
+def dot_table(values, high, low):
+    rows = values.shape[0]
+    large, small = parts(values, 2)
+    sums = dot(jnp.concatenate([large, small], axis=0), high)
+    return sums[:rows] + (sums[rows:] + dot(large, low))
 
 
 def lanes_of(rows):
@@ -100,15 +128,17 @@
 
 
 def advance_body(
-    downflow, shear, counts, cells, far_table, far_fields, far_cells,
-    out, start, first, second, table, sort_fields, sort_cells, done,
+    downflow, shear, counts, cells, far_table, far_synth, far_fields, far_cells,
+    out, start, first, second, table, synth, sort_fields, sort_cells, done,
 ):
     fetch_table = pltpu.make_async_copy(far_table, table, done.at[0])
     fetch_fields = pltpu.make_async_copy(far_fields, sort_fields, done.at[1])
     fetch_cells = pltpu.make_async_copy(far_cells, sort_cells, done.at[2])
+    fetch_synth = pltpu.make_async_copy(far_synth, synth, done.at[3])
     fetch_cells.start()
     fetch_table.start()
     fetch_fields.start()
+    fetch_synth.start()
     chunk = 64
     edge = 8
     lane = lanes_of(chunk)
@@ -173,7 +203,7 @@
         fields = jnp.where(part == 0, last, 0.0)
         fields = jnp.where(part == 1, roll(last * last, 4, 1), fields)
         first[row : row + chunk] = jnp.where(part == 2, roll(last * other, 8, 1), fields)
-        sorted_cells = dot(jnp.where(part == 0, last, 0.0), sort_cells[...])
+        sorted_cells = picked(jnp.where(part == 0, last, 0.0), sort_cells[...])
         sorted_cells = sorted_cells.reshape(chunk // 16, 2, 8, LANES)
         side = lax.broadcasted_iota(jnp.int32, (chunk // 16, 8, LANES), 2)
         out[row // 16 : (row + chunk) // 16, 16:24] = jnp.where(
@@ -181,7 +211,7 @@
         )
     fetch_table.wait()
     fetch_fields.wait()
-    coeffs = dot(dot(table[...], first[:NZ]), sort_fields[...])
+    coeffs = picked(table_dot(table[0], table[1], first[:NZ]), sort_fields[...])
     mode = lax.broadcasted_iota(jnp.int32, (MODES, LANES), 0)
     number = jnp.where(mode < HALF, mode, mode - HALF + 1)
     plane = lanes_of(MODES) % 32 % PLANES
@@ -190,7 +220,8 @@
         limit = jnp.where(plane == p, counts[1, p], limit)
     weight = jnp.where(mode == 0, 1.0 / NZ, 2.0 / NZ)
     coeffs = jnp.where(number <= limit, coeffs * weight, 0.0)
-    out[:, 0:16] = dot(table[...].T, coeffs).reshape(GZ, 16, LANES)
+    fetch_synth.wait()
+    out[:, 0:16] = table_dot(synth[0], synth[1], coeffs).reshape(GZ, 16, LANES)
 
 
 def forward_body(cells, out):
@@ -201,7 +232,7 @@
 def unsort():
     source = lax.broadcasted_iota(jnp.int32, (LANES, LANES), 0)
     target = lax.broadcasted_iota(jnp.int32, (LANES, LANES), 1)
-    return jnp.where(target == source % 32 * 4 + source // 32, 1.0, 0.0)
+    return jnp.where(target == source % 32 * 4 + source // 32, 1.0, 0.0).astype(jnp.bfloat16)
 
 
 def cells_body(cells, out, rows):
@@ -221,7 +252,7 @@
                     joined = jnp.where(lane // 32 == column, moved, joined)
                 place = (half * 8 + group * 4 + r) * 16
                 rows[place : place + 16] = joined
-    rows[...] = dot(rows[...], order)
+    rows[...] = picked(rows[...], order)
     for c in range(3):
         for p in range(PLANES):
             out[c, p] = rows[pl.ds(c * PLANES + p, TILE_Z, stride=16), :]
@@ -236,10 +267,12 @@
         fetch.start()
     cells = lines[...].reshape(NX // 4, LANES)
     fetches[0].wait()
-    coeffs = dot(table[0], cells)
+    coeffs = table_dot(table[0, 0], table[0, 1], cells)
     for column in range(1, 4):
         fetches[column].wait()
-        coeffs = coeffs + roll(dot(table[column], cells), -32 * column, 1)
+        coeffs = coeffs + roll(
+            table_dot(table[column, 0], table[column, 1], cells), -32 * column, 1
+        )
     mode = lax.broadcasted_iota(jnp.int32, (MODES, LANES), 0)
     number = jnp.where(mode < HALF, mode, mode - HALF + 1)
     weight = jnp.where(mode == 0, 1.0 / NX, 2.0 / NX)
@@ -250,7 +283,7 @@
     coeffs = jnp.where(number <= limit, coeffs * weight, 0.0).T[:32]
     rows[...] = jnp.zeros(rows.shape, jnp.float32)
     for column in range(4):
-        filtered = dot(coeffs, table[column])
+        filtered = dot_table(coeffs, table[column, 0], table[column, 1])
         for q, (a, b) in enumerate(zip(pair_first, pair_second)):
             rows[column, 3 * q : 3 * q + 3] = (
                 filtered[9 + 3 * q : 12 + 3 * q]
@@ -267,7 +300,7 @@
 
 
 def stress_body(lines, out, rows):
-    rows[...] = dot(lines[...].reshape(16 * 24, LANES), unsort())
+    rows[...] = picked(lines[...].reshape(16 * 24, LANES), unsort())
     for q in range(6):
         for p in range(PLANES):
             out[q, p] = rows[pl.ds(q * PLANES + p, TILE_Z, stride=24), :]
@@ -295,9 +328,21 @@
                     sort_fields[lane + 4 * kind, column * 32 + field] = 1.0
                 for half in range(2):
                     sort_cells[lane, half * 64 + column * 16 + c * PLANES + p] = 1.0
+
+    def halves(values):
+        high = values.astype(jnp.bfloat16)
+        low = (values - high.astype(np.float64)).astype(jnp.bfloat16)
+        return np.stack([high, low], axis=-3)
+
     return [
-        jnp.asarray(np.ascontiguousarray(values, dtype=np.float32))
-        for values in (synth_z, sort_fields, sort_cells, synth_x)
+        jnp.asarray(np.ascontiguousarray(values))
+        for values in (
+            halves(synth_z),
+            halves(synth_z.T),
+            sort_fields.astype(jnp.bfloat16),
+            sort_cells.astype(jnp.bfloat16),
+            halves(synth_x),
+        )
     ]
 
 
@@ -306,7 +351,7 @@
     mode_counts = mode_counts.T
     left = lax.ppermute(velocity, "gx", [(i, (i + 1) % count) for i in range(count)])
     right = lax.ppermute(velocity, "gx", [((i + 1) % count, i) for i in range(count)])
-    synth_z, sort_fields, sort_cells, synth_x = wave_tables()
+    analysis_z, synth_z, sort_fields, sort_cells, synth_x = wave_tables()
     (inner,) = call(inner_body, [(GZ, TILE_Z, LANES)], 0, [], velocity)
     (cells,) = call(
         outer_body,
@@ -329,10 +374,11 @@
         shear,
         mode_counts,
         cells,
+        analysis_z,
         synth_z,
         sort_fields,
         sort_cells,
-        tables=3,
+        tables=4,
     )
     cells = lax.all_to_all(cells, spanwise, 0, 0, tiled=True)
     (lines,) = call(forward_body, [(GX, GZ, LANES)], 0, [], cells)

time: 96.3 us -> 92.5 us (0.961)
  Pallas kernels: 15.3 us -> 11.4 us
    pallas_call x7, Pallas kernels: 15.3 us -> 11.4 us  [call(): pl.pallas_call(body, out_shape=[make(shape, jnp.float32) for shape in out...]
where the time goes in v4:
time: 92.5 us; the launch traced here: 92.1 us
  blocking collectives  59.9 us (65%)
  Pallas kernels  11.4 us (12%)
  starting transfers between devices  10.3 us (11%)
  waiting for transfers between devices  8.87 us (10%)
    all_to_all x2, blocking collectives, local(): cells = lax.all_to_all(cells, spanwise, 0, 0, tiled=True)  34.8 us
    all_to_all x1, blocking collectives, local(): lines = lax.all_to_all(lines, 'gx', 0, 0, tiled=True)  25.2 us
    pallas_call x7, Pallas kernels, call(): pl.pallas_call(body, out_shape=[make(shape, jnp.float32) for shape in out...  11.4 us
    all_to_all x1, waiting for transfers between devices, local(): lines = lax.all_to_all(lines, 'gx', 0, 0, tiled=True)  8.7 us
    ppermute x1, starting transfers between devices, local(): lax.ppermute(velocity, 'gx', [((i + 1) % count, i) for i in range(count)])  6.85 us
    all_to_all x1, starting transfers between devices, local(): lines = lax.all_to_all(lines, 'gx', 0, 0, tiled=True)  3.43 us
  transfers between devices with their start and end apart: 3, of which 2 were waited for; matrix products, arithmetic and copies ran while one was open for 0% of the time, Pallas kernels for 2%

profile of v4, /device:TPU:1, one launch (start us, length us, event | category | flops | bytes accessed | tf_op | source)
XLA Modules:
  0.0 92.1 jit_solution(11705206450276810069)
XLA Ops:
  0.6 6.9 %collective-permute-start.1 = (f32[3,3,16,128]{3,2,1,0:T(8,128)}, f32[3,3,16,128]{3,2,1,0:T(8,128)S(1)}, u32[]{:S(2)}, u32[]{:S(2)}) collective-permute-start(f32[3,3,16,128]{3,2,1,0:T(8,128)} %own.3), channel_id=1, source_target_pairs={{32,0},{64,32},{96,64},{128,96},{160,128},{192,160},{224,192},{256... | collective-permute-start | bytes 221192 | tf_op jit(solution)/shard_map/ppermute | solution.py:353
  7.5 0.0 collective-permute-start
  7.5 0.0 copy-start
  7.5 0.9 copy-done
  8.4 0.6 shard_map.104.inner
  9.0 0.0 collective-permute-done.1.right
  9.0 0.2 collective-permute-done.left
  9.2 0.1 shard_map.105
  9.3 19.7 %all_to_all.20.cells = f32[32,16,128]{2,1,0:T(8,128)S(1)} all-to-all(f32[32,16,128]{2,1,0:T(8,128)S(1)} %shard_map.105), channel_id=1, replica_groups=mesh['gx'=16,'gz'=16,'grp'=2] {'gz','grp'}, dimensions={0} | all-to-all | bytes 524288 | tf_op jit(solution)/shard_map/all_to_all | solution.py:367
  29.0 4.1 %shard_map.106 = f32[32,24,128]{2,1,0:T(8,128)S(1)} custom-call(f32[3]{0:T(128)} %downflow.1, f32[3]{0:T(128)} %shear.1, s32[2,3]{1,0:T(2,128)} %bitcast.1, f32[32,16,128]{2,1,0:T(8,128)S(1)} %all_to_all.20.cells, bf16[2,256,512]{2,1,0:T(8,128)(2,1)} %constant.10.clone.far_table, bf16[2,512,256]{2,1,0:T(8,128)(2,1)} %constant.11.clone.far_synth, ...), custom_call_target="tpu_custom_call" | custom-call | tf_op jit(solution)/shard_map/pallas_call | solution.py:46
  33.1 15.1 %all_to_all.21.cells = f32[32,24,128]{2,1,0:T(8,128)S(1)} all-to-all(f32[32,24,128]{2,1,0:T(8,128)S(1)} %shard_map.106), channel_id=1, replica_groups=mesh['gx'=16,'gz'=16,'grp'=2] {'gz','grp'}, dimensions={0} | all-to-all | bytes 786432 | tf_op jit(solution)/shard_map/all_to_all | solution.py:383
  48.2 0.1 shard_map.108
  48.3 25.2 %all_to_all.22.lines = f32[16,32,128]{2,1,0:T(8,128)S(1)} all-to-all(f32[16,32,128]{2,1,0:T(8,128)S(1)} %shard_map.108), channel_id=1, replica_groups=mesh['gx'=16,'gz'=16,'grp'=2] {'gx'}, dimensions={0} | all-to-all | bytes 524288 | tf_op jit(solution)/shard_map/all_to_all | solution.py:385
  73.5 4.4 %shard_map.109 = f32[16,24,128]{2,1,0:T(8,128)} custom-call(s32[2,3]{1,0:T(2,128)} %bitcast.2, f32[16,32,128]{2,1,0:T(8,128)S(1)} %all_to_all.22.lines, bf16[4,2,256,512]{3,2,1,0:T(8,128)(2,1)} %constant.14.clone.far_table), custom_call_target="tpu_custom_call" | custom-call | tf_op jit(solution)/shard_map/pallas_call | solution.py:46
  77.9 3.4 %all-to-all-start.3 = ((f32[16,24,128]{2,1,0:T(8,128)}), f32[16,24,128]{2,1,0:T(8,128)S(1)}, u32[]{:S(2)}, u32[]{:S(2)}) async-start(f32[16,24,128]{2,1,0:T(8,128)} %shard_map.109), calls=%async_computation.3 | async-start | bytes 393216 | tf_op jit(solution)/shard_map/all_to_all | solution.py:399
  81.4 1.1 %shard_map.107 = f32[3,3,16,128]{3,2,1,0:T(8,128)} custom-call(f32[32,24,128]{2,1,0:T(8,128)S(1)} %all_to_all.21.cells), custom_call_target="tpu_custom_call" | custom-call | tf_op jit(solution)/shard_map/pallas_call | solution.py:46
  82.4 8.7 %all-to-all-done.3.lines = f32[16,24,128]{2,1,0:T(8,128)S(1)} async-done(((f32[16,24,128]{2,1,0:T(8,128)}), f32[16,24,128]{2,1,0:T(8,128)S(1)}, u32[]{:S(2)}, u32[]{:S(2)}) %all-to-all-start.3) | async-done | bytes 196640 | tf_op jit(solution)/shard_map/all_to_all | solution.py:399
  91.1 0.9 shard_map.110
Async XLA Ops:
  0.6 8.4 %collective-permute-start.1 = (f32[3,3,16,128]{3,2,1,0:T(8,128)}, f32[3,3,16,128]{3,2,1,0:T(8,128)S(1)}, u32[]{:S(2)}, u32[]{:S(2)}) collective-permute-start(f32[3,3,16,128]{3,2,1,0:T(8,128)} %own.3), channel_id=1, source_target_pairs={{32,0},{64,32},{96,64},{128,96},{160,128},{192,160},{224,192},{256... | collective-permute-start | bytes 221192 | tf_op jit(solution)/shard_map/ppermute | solution.py:353
  7.5 1.7 %collective-permute-start = (f32[3,3,16,128]{3,2,1,0:T(8,128)}, f32[3,3,16,128]{3,2,1,0:T(8,128)S(1)}, u32[]{:S(2)}, u32[]{:S(2)}) collective-permute-start(f32[3,3,16,128]{3,2,1,0:T(8,128)} %own.3), channel_id=1, source_target_pairs={{0,32},{32,64},{64,96},{96,128},{128,160},{160,192},{192,224},{224... | collective-permute-start | bytes 221192 | tf_op jit(solution)/shard_map/ppermute | solution.py:352
  7.5 0.9 copy-start
  77.9 13.2 %all-to-all-start.3 = ((f32[16,24,128]{2,1,0:T(8,128)}), f32[16,24,128]{2,1,0:T(8,128)S(1)}, u32[]{:S(2)}, u32[]{:S(2)}) async-start(f32[16,24,128]{2,1,0:T(8,128)} %shard_map.109), calls=%async_computation.3 | async-start | bytes 393216 | tf_op jit(solution)/shard_map/all_to_all | solution.py:399

commit v5 on v4

--- a/solution.py
+++ b/solution.py
@@ -21,6 +21,9 @@
 
 SLOT = 14
 STRIDE = PLANES * SLOT
+FIELDS = 9 * PLANES
+BACK = 18
+STRESSES = 6 * PLANES
 
 molecular_diffusivity = 0.4
 time_step = 0.2
@@ -192,6 +195,7 @@
         middle, change = rate(first, row)
         begin = start[edge + row : edge + row + chunk]
         store(second, row, 0.75 * begin + 0.25 * (middle + time_step * change))
+    in_eight = lax.broadcasted_iota(jnp.int32, (chunk, LANES), 0) % 8
     fetch_cells.wait()
     part = (lane + LANES - 3) % LANES % SLOT // 4
     part = jnp.where((lane >= 3) & (lane < 127), part, 3)
@@ -204,29 +208,32 @@
         fields = jnp.where(part == 1, roll(last * last, 4, 1), fields)
         first[row : row + chunk] = jnp.where(part == 2, roll(last * other, 8, 1), fields)
         sorted_cells = picked(jnp.where(part == 0, last, 0.0), sort_cells[...])
-        sorted_cells = sorted_cells.reshape(chunk // 16, 2, 8, LANES)
-        side = lax.broadcasted_iota(jnp.int32, (chunk // 16, 8, LANES), 2)
-        out[row // 16 : (row + chunk) // 16, 16:24] = jnp.where(
-            side < LANES // 2, sorted_cells[:, 0], sorted_cells[:, 1]
-        )
+        start[edge + row : edge + row + chunk] = sorted_cells[:, :LANES]
+        rest = jnp.where(lane // 16 == in_eight, sorted_cells[:, LANES:], 0.0)
+        rest = jnp.sum(rest.reshape(chunk // 8, 8, LANES), axis=1)
+        for block in range(chunk // 16):
+            place = (row // 16 + block) * BACK + 16
+            out[place : place + 2] = rest[2 * block : 2 * block + 2]
     fetch_table.wait()
     fetch_fields.wait()
     coeffs = picked(table_dot(table[0], table[1], first[:NZ]), sort_fields[...])
     mode = lax.broadcasted_iota(jnp.int32, (MODES, LANES), 0)
     number = jnp.where(mode < HALF, mode, mode - HALF + 1)
-    plane = lanes_of(MODES) % 32 % PLANES
+    plane = lanes_of(MODES) % PLANES
     limit = jnp.zeros((MODES, LANES), jnp.int32)
     for p in range(PLANES):
         limit = jnp.where(plane == p, counts[1, p], limit)
     weight = jnp.where(mode == 0, 1.0 / NZ, 2.0 / NZ)
     coeffs = jnp.where(number <= limit, coeffs * weight, 0.0)
     fetch_synth.wait()
-    out[:, 0:16] = table_dot(synth[0], synth[1], coeffs).reshape(GZ, 16, LANES)
+    filtered = table_dot(synth[0], synth[1], coeffs) + start[edge : edge + NZ]
+    for block in range(GZ):
+        out[block * BACK : block * BACK + 16] = filtered[16 * block : 16 * block + 16]
 
 
 def forward_body(cells, out):
     for row in range(TILE_Z):
-        out[row] = cells[:, row, :]
+        out[row] = cells[pl.ds(row, GZ, stride=BACK), :]
 
 
 def unsort():
@@ -236,22 +243,29 @@
 
 
 def cells_body(cells, out, rows):
-    lane = lanes_of(16)
+    lane = lanes_of(8)
+    rest = jnp.concatenate(
+        [cells[pl.ds(16 + half, GZ, stride=BACK), :] for half in range(2)] * 2, axis=0
+    ).T
+    for group in range(4):
+        turned = jnp.concatenate(
+            [cells[pl.ds(4 * group + r, GZ, stride=BACK), :] for r in range(4)], axis=0
+        ).T
+        for r in range(4):
+            row = 4 * group + r
+            for begin, source, count, at in (
+                (4 * FIELDS, turned, 5, r),
+                (row % 8 * 16, rest, 4, row // 8),
+            ):
+                joined = jnp.zeros((count, LANES), jnp.float32)
+                for column in range(4):
+                    low = begin + column * count
+                    moved = roll(source[low : low + count], (column - at) * 32, 1)
+                    joined = jnp.where(lane[:count] // 32 == column, moved, joined)
+                place = row * 16 + (0 if count == 5 else 5)
+                rows[place : place + count] = joined
+            rows[row * 16 + 9 : row * 16 + 16] = jnp.zeros((7, LANES), jnp.float32)
     order = unsort()
-    for group in range(2):
-        stacked = jnp.concatenate(
-            [cells[:, 16 + 4 * group + r, :] for r in range(4)], axis=0
-        )
-        turned = stacked.T
-        for half in range(2):
-            for r in range(4):
-                joined = jnp.zeros((16, LANES), jnp.float32)
-                for column in range(4):
-                    begin = half * 64 + column * 16
-                    moved = roll(turned[begin : begin + 16], (column - r) * 32, 1)
-                    joined = jnp.where(lane // 32 == column, moved, joined)
-                place = (half * 8 + group * 4 + r) * 16
-                rows[place : place + 16] = joined
     rows[...] = picked(rows[...], order)
     for c in range(3):
         for p in range(PLANES):
@@ -271,7 +285,7 @@
     for column in range(1, 4):
         fetches[column].wait()
         coeffs = coeffs + roll(
-            table_dot(table[column, 0], table[column, 1], cells), -32 * column, 1
+            table_dot(table[column, 0], table[column, 1], cells), -FIELDS * column, 1
         )
     mode = lax.broadcasted_iota(jnp.int32, (MODES, LANES), 0)
     number = jnp.where(mode < HALF, mode, mode - HALF + 1)
@@ -279,7 +293,7 @@
     lane = lanes_of(MODES)
     limit = jnp.full((MODES, LANES), -1, jnp.int32)
     for p in range(PLANES):
-        limit = jnp.where((lane < 27) & (lane % PLANES == p), counts[0, p], limit)
+        limit = jnp.where((lane < FIELDS) & (lane % PLANES == p), counts[0, p], limit)
     coeffs = jnp.where(number <= limit, coeffs * weight, 0.0).T[:32]
     rows[...] = jnp.zeros(rows.shape, jnp.float32)
     for column in range(4):
@@ -296,14 +310,14 @@
         for column in range(4):
             moved = roll(rows[column, :, begin : begin + LANES], (column - dest % 4) * 32, 1)
             joined = jnp.where(lane // 32 == column, moved, joined)
-        out[dest] = joined
+        out[dest * STRESSES : (dest + 1) * STRESSES] = joined[:STRESSES]
 
 
 def stress_body(lines, out, rows):
-    rows[...] = picked(lines[...].reshape(16 * 24, LANES), unsort())
+    rows[...] = picked(lines[...], unsort())
     for q in range(6):
         for p in range(PLANES):
-            out[q, p] = rows[pl.ds(q * PLANES + p, TILE_Z, stride=24), :]
+            out[q, p] = rows[pl.ds(q * PLANES + p, TILE_Z, stride=STRESSES), :]
 
 
 def wave_table(length):
@@ -317,7 +331,7 @@
     synth_z = wave_table(NZ).T
     synth_x = wave_table(NX).reshape(NX // 4, 4, MODES).transpose(1, 2, 0)
     sort_fields = np.zeros((LANES, LANES))
-    sort_cells = np.zeros((LANES, LANES))
+    sort_cells = np.zeros((LANES, 2 * LANES))
     kinds = ((0, 1, 2), (3, 6, 8), (4, 7, 5))
     for c in range(3):
         for p in range(PLANES):
@@ -325,9 +339,13 @@
                 lane = c * STRIDE + p * SLOT + 3 + column
                 for kind in range(3):
                     field = kinds[kind][c] * PLANES + p
-                    sort_fields[lane + 4 * kind, column * 32 + field] = 1.0
-                for half in range(2):
-                    sort_cells[lane, half * 64 + column * 16 + c * PLANES + p] = 1.0
+                    sort_fields[lane + 4 * kind, column * FIELDS + field] = 1.0
+                index = c * PLANES + p
+                if index < 5:
+                    sort_cells[lane, 4 * FIELDS + column * 5 + index] = 1.0
+                else:
+                    begin = LANES + column * 4 + index - 5
+                    sort_cells[lane, begin : 2 * LANES : 16] = 1.0
 
     def halves(values):
         high = values.astype(jnp.bfloat16)
@@ -344,6 +362,11 @@
             halves(synth_x),
         )
     ]
+
+
+def exchange(rows, axis, count):
+    sent = rows.reshape(count, -1, 2, LANES)
+    return lax.all_to_all(sent, axis, 0, 0, tiled=True).reshape(rows.shape)
 
 
 def local(velocity, downflow, shear, mode_counts):
@@ -367,7 +390,7 @@
     cells = lax.all_to_all(cells, spanwise, 0, 0, tiled=True)
     (cells,) = call(
         advance_body,
-        [(GZ, 24, LANES)],
+        [(GZ * BACK, LANES)],
         3,
         [(NZ + 16, LANES)] * 3,
         downflow,
@@ -380,7 +403,7 @@
         sort_cells,
         tables=4,
     )
-    cells = lax.all_to_all(cells, spanwise, 0, 0, tiled=True)
+    cells = exchange(cells, spanwise, GZ)
     (lines,) = call(forward_body, [(GX, GZ, LANES)], 0, [], cells)
     lines = lax.all_to_all(lines, "gx", 0, 0, tiled=True)
     (advanced,) = call(
@@ -388,7 +411,7 @@
     )
     (lines,) = call(
         streamwise_body,
-        [(GX, 24, LANES)],
+        [(GX * STRESSES, LANES)],
         1,
         [(4, 24, NX // 4)],
         mode_counts,
@@ -396,9 +419,9 @@
         synth_x,
         tables=1,
     )
-    lines = lax.all_to_all(lines, "gx", 0, 0, tiled=True)
+    lines = exchange(lines, "gx", GX)
     (stress,) = call(
-        stress_body, [(6, PLANES, TILE_Z, TILE_X)], 0, [(16 * 24, LANES)], lines, final=True
+        stress_body, [(6, PLANES, TILE_Z, TILE_X)], 0, [(GX * STRESSES, LANES)], lines, final=True
     )
     return advanced, stress
 

time: 92.5 us -> 89.3 us (0.965)
  blocking collectives: 59.9 us -> 58.1 us
  waiting for transfers between devices: 8.87 us -> 7.74 us
    all_to_all x2 -> x1, blocking collectives: 34.8 us -> 19.7 us  [local(): cells = lax.all_to_all(cells, spanwise, 0, 0, tiled=True)]
    all_to_all x0 -> x1, blocking collectives: none -> 14.2 us  [exchange(): return lax.all_to_all(sent, axis, 0, 0, tiled=True).reshape(rows.shape)]
    all_to_all x1, waiting for transfers between devices: 8.7 us -> 7.58 us  [exchange(): return lax.all_to_all(sent, axis, 0, 0, tiled=True).reshape(rows.shape)]
    all_to_all x1, blocking collectives: 25.2 us -> 24.2 us  [local(): lines = lax.all_to_all(lines, 'gx', 0, 0, tiled=True)]
where the time goes in v5:
time: 89.3 us; the launch traced here: 88.9 us
  blocking collectives  58.1 us (65%)
  Pallas kernels  11.2 us (13%)
  starting transfers between devices  10.3 us (12%)
  waiting for transfers between devices  7.74 us (9%)
  local copies, waits for them, and re-layouts  0.92 us (1%)
    all_to_all x1, blocking collectives, local(): lines = lax.all_to_all(lines, 'gx', 0, 0, tiled=True)  24.2 us
    all_to_all x1, blocking collectives, local(): cells = lax.all_to_all(cells, spanwise, 0, 0, tiled=True)  19.7 us
    all_to_all x1, blocking collectives, exchange(): return lax.all_to_all(sent, axis, 0, 0, tiled=True).reshape(rows.shape)  14.2 us
    pallas_call x7, Pallas kernels, call(): pl.pallas_call(body, out_shape=[make(shape, jnp.float32) for shape in out...  11.2 us
    all_to_all x1, waiting for transfers between devices, exchange(): return lax.all_to_all(sent, axis, 0, 0, tiled=True).reshape(rows.shape)  7.58 us
    ppermute x1, starting transfers between devices, local(): lax.ppermute(velocity, 'gx', [((i + 1) % count, i) for i in range(count)])  6.85 us
    all_to_all x1, starting transfers between devices, exchange(): return lax.all_to_all(sent, axis, 0, 0, tiled=True).reshape(rows.shape)  3.42 us
  transfers between devices with their start and end apart: 3, of which 2 were waited for; matrix products, arithmetic and copies ran while one was open for 0% of the time, Pallas kernels for 2%

profile of v5, /device:TPU:1, one launch (start us, length us, event | category | flops | bytes accessed | tf_op | source)
XLA Modules:
  0.0 88.9 jit_solution(11249562192367550627)
XLA Ops:
  0.6 6.9 %collective-permute-start.1 = (f32[3,3,16,128]{3,2,1,0:T(8,128)}, f32[3,3,16,128]{3,2,1,0:T(8,128)S(1)}, u32[]{:S(2)}, u32[]{:S(2)}) collective-permute-start(f32[3,3,16,128]{3,2,1,0:T(8,128)} %own.3), channel_id=1, source_target_pairs={{32,0},{64,32},{96,64},{128,96},{160,128},{192,160},{224,192},{256... | collective-permute-start | bytes 221192 | tf_op jit(solution)/shard_map/ppermute | solution.py:376
  7.5 0.0 collective-permute-start
  7.5 0.0 copy-start
  7.5 0.9 %copy-done = f32[3,3,16,128]{3,2,1,0:T(8,128)S(1)} copy-done((f32[3,3,16,128]{3,2,1,0:T(8,128)S(1)}, f32[3,3,16,128]{3,2,1,0:T(8,128)}, u32[]{:S(2)}) %copy-start) | copy-done | bytes 73752
  8.4 0.6 shard_map.104.inner
  9.0 0.0 collective-permute-done.1.right
  9.0 0.2 collective-permute-done.left
  9.2 0.1 shard_map.105
  9.3 19.7 %all_to_all.20.cells = f32[32,16,128]{2,1,0:T(8,128)S(1)} all-to-all(f32[32,16,128]{2,1,0:T(8,128)S(1)} %shard_map.105), channel_id=1, replica_groups=mesh['gx'=16,'gz'=16,'grp'=2] {'gz','grp'}, dimensions={0} | all-to-all | bytes 524288 | tf_op jit(solution)/shard_map/all_to_all | solution.py:390
  29.0 4.0 %shard_map.106 = f32[576,128]{1,0:T(8,128)S(1)} custom-call(f32[3]{0:T(128)} %downflow.1, f32[3]{0:T(128)} %shear.1, s32[2,3]{1,0:T(2,128)} %bitcast.9, f32[32,16,128]{2,1,0:T(8,128)S(1)} %all_to_all.20.cells, bf16[2,256,512]{2,1,0:T(8,128)(2,1)} %constant.10.clone.far_table, bf16[2,512,256]{2,1,0:T(8,128)(2,1)} %constant.11.clone.far_synth, ...), custom_call_target="tpu_custom_call" | custom-call | tf_op jit(solution)/shard_map/pallas_call | solution.py:49
  33.0 14.2 %all_to_all.21 = f32[32,9,2,128]{3,2,1,0:T(2,128)S(1)} all-to-all(f32[32,9,2,128]{3,2,1,0:T(2,128)S(1)} %bitcast.7), channel_id=1, replica_groups=mesh['gx'=16,'gz'=16,'grp'=2] {'gz','grp'}, dimensions={0} | all-to-all | bytes 589824 | tf_op jit(solution)/shard_map/all_to_all | solution.py:369
  47.3 24.2 %all_to_all.22.lines = f32[16,32,128]{2,1,0:T(8,128)S(1)} all-to-all(f32[16,32,128]{2,1,0:T(8,128)S(1)} %shard_map.108), channel_id=1, replica_groups=mesh['gx'=16,'gz'=16,'grp'=2] {'gx'}, dimensions={0} | all-to-all | bytes 524288 | tf_op jit(solution)/shard_map/all_to_all | solution.py:408
  71.5 4.4 %shard_map.109 = f32[288,128]{1,0:T(8,128)} custom-call(s32[2,3]{1,0:T(2,128)} %bitcast.10, f32[16,32,128]{2,1,0:T(8,128)S(1)} %all_to_all.22.lines, bf16[4,2,256,512]{3,2,1,0:T(8,128)(2,1)} %constant.14.clone.far_table), custom_call_target="tpu_custom_call" | custom-call | tf_op jit(solution)/shard_map/pallas_call | solution.py:49
  75.9 3.4 %all-to-all-start.3 = ((f32[16,9,2,128]{3,2,1,0:T(2,128)}), f32[16,9,2,128]{3,2,1,0:T(2,128)S(1)}, u32[]{:S(2)}, u32[]{:S(2)}) async-start(f32[16,9,2,128]{3,2,1,0:T(2,128)} %bitcast.3), calls=%async_computation.3 | async-start | bytes 294912 | tf_op jit(solution)/shard_map/all_to_all | solution.py:369
  79.3 1.2 %shard_map.107 = f32[3,3,16,128]{3,2,1,0:T(8,128)} custom-call(f32[576,128]{1,0:T(8,128)S(1)} %bitcast.6), custom_call_target="tpu_custom_call" | custom-call | tf_op jit(solution)/shard_map/pallas_call | solution.py:49
  80.5 7.6 %all-to-all-done.3 = f32[16,9,2,128]{3,2,1,0:T(2,128)S(1)} async-done(((f32[16,9,2,128]{3,2,1,0:T(2,128)}), f32[16,9,2,128]{3,2,1,0:T(2,128)S(1)}, u32[]{:S(2)}, u32[]{:S(2)}) %all-to-all-start.3) | async-done | bytes 147488 | tf_op jit(solution)/shard_map/all_to_all | solution.py:369
  88.0 0.9 shard_map.110
  (1 shorter events, 0.0 us)
Async XLA Ops:
  0.6 8.4 %collective-permute-start.1 = (f32[3,3,16,128]{3,2,1,0:T(8,128)}, f32[3,3,16,128]{3,2,1,0:T(8,128)S(1)}, u32[]{:S(2)}, u32[]{:S(2)}) collective-permute-start(f32[3,3,16,128]{3,2,1,0:T(8,128)} %own.3), channel_id=1, source_target_pairs={{32,0},{64,32},{96,64},{128,96},{160,128},{192,160},{224,192},{256... | collective-permute-start | bytes 221192 | tf_op jit(solution)/shard_map/ppermute | solution.py:376
  7.5 1.7 %collective-permute-start = (f32[3,3,16,128]{3,2,1,0:T(8,128)}, f32[3,3,16,128]{3,2,1,0:T(8,128)S(1)}, u32[]{:S(2)}, u32[]{:S(2)}) collective-permute-start(f32[3,3,16,128]{3,2,1,0:T(8,128)} %own.3), channel_id=1, source_target_pairs={{0,32},{32,64},{64,96},{96,128},{128,160},{160,192},{192,224},{224... | collective-permute-start | bytes 221192 | tf_op jit(solution)/shard_map/ppermute | solution.py:375
  7.5 0.9 %copy-start = (f32[3,3,16,128]{3,2,1,0:T(8,128)S(1)}, f32[3,3,16,128]{3,2,1,0:T(8,128)}, u32[]{:S(2)}) copy-start(f32[3,3,16,128]{3,2,1,0:T(8,128)} %own.3) | copy-start | bytes 221188
  75.9 12.2 %all-to-all-start.3 = ((f32[16,9,2,128]{3,2,1,0:T(2,128)}), f32[16,9,2,128]{3,2,1,0:T(2,128)S(1)}, u32[]{:S(2)}, u32[]{:S(2)}) async-start(f32[16,9,2,128]{3,2,1,0:T(2,128)} %bitcast.3), calls=%async_computation.3 | async-start | bytes 294912 | tf_op jit(solution)/shard_map/all_to_all | solution.py:369

commit v6 on v5

--- a/solution.py
+++ b/solution.py
@@ -41,21 +41,25 @@
     make = jax.ShapeDtypeStruct if final else pltpu.VMEM
     near = len(args) - tables
     args = (
-        args[:smem]
+        tuple(pltpu.with_memory_space_constraint(arg, pltpu.HBM) for arg in args[:smem])
         + tuple(pltpu.with_memory_space_constraint(arg, pltpu.VMEM) for arg in args[smem:near])
-        + args[near:]
-    )
-    fetched = [pltpu.VMEM(arg.shape, arg.dtype) for arg in args[near:]]
+        + tuple(pltpu.with_memory_space_constraint(arg, pltpu.HBM) for arg in args[near:])
+    )
     return pl.pallas_call(
         body,
-        out_shape=[make(shape, jnp.float32) for shape in out_shapes],
+        out_shape=[
+            make(shape.shape, shape.dtype)
+            if isinstance(shape, jax.Array)
+            else make(shape, jnp.float32)
+            for shape in out_shapes
+        ],
         in_specs=[pl.BlockSpec(memory_space=pltpu.SMEM)] * smem
         + [pl.BlockSpec(memory_space=pltpu.VMEM)] * (near - smem)
-        + [pl.BlockSpec(memory_space=pl.ANY)] * tables,
+        + [pl.BlockSpec(memory_space=pltpu.HBM)] * tables,
         out_specs=[pl.BlockSpec(memory_space=pltpu.VMEM)] * len(out_shapes),
         scratch_shapes=[pltpu.VMEM(shape, jnp.float32) for shape in scratch]
-        + fetched
-        + ([pltpu.SemaphoreType.DMA((4,))] if tables else []),
+        + ([pltpu.SemaphoreType.DMA((tables,))] if tables else []),
+        compiler_params=pltpu.CompilerParams(vmem_limit_bytes=16 << 20),
         input_output_aliases=alias or {},
     )(*args)
 
@@ -113,12 +117,43 @@
     return packed
 
 
-def inner_body(own, out):
-    cells = [own[c, p] for c in range(3) for p in range(PLANES)]
+def inner_body(downflow, shear, counts, *refs):
+    far = refs[:6]
+    out, flow, slope, mask_z, mask_x = refs[6:11]
+    near = refs[11:17]
+    done = refs[17]
+    fetches = [
+        pltpu.make_async_copy(source, target, done.at[index])
+        for index, (source, target) in enumerate(zip(far, near))
+    ]
+    for fetch in fetches:
+        fetch.start()
+    fetches[0].wait()
+    cells = [near[0][c, p] for c in range(3) for p in range(PLANES)]
     for dest in range(1, GZ - 1):
         out[dest] = packed_for(dest, cells)
     out[0] = packed_for(GZ // 2, cells)
     out[GZ - 1] = packed_for(GZ // 2, cells)
+    lane = lanes_of(8)
+    plane = lane % STRIDE // SLOT
+    speeds = jnp.zeros((8, LANES), jnp.float32)
+    shears = jnp.zeros((8, LANES), jnp.float32)
+    for p in range(PLANES):
+        speeds = jnp.where(plane == p, downflow[p], speeds)
+        shears = jnp.where((plane == p) & (lane < STRIDE), shear[p], shears)
+    flow[...] = speeds
+    slope[...] = shears
+    mode = lax.broadcasted_iota(jnp.int32, (MODES, LANES), 0)
+    number = jnp.where(mode < HALF, mode, mode - HALF + 1)
+    plane = lanes_of(MODES) % PLANES
+    for mask, axis, length in ((mask_z, 1, NZ), (mask_x, 0, NX)):
+        limit = jnp.zeros((MODES, LANES), jnp.int32)
+        for p in range(PLANES):
+            limit = jnp.where(plane == p, counts[axis, p], limit)
+        weight = jnp.where(mode == 0, 1.0 / length, 2.0 / length)
+        mask[...] = jnp.where(number <= limit, weight, 0.0)
+    for fetch in fetches[1:]:
+        fetch.wait()
 
 
 def outer_body(own, left, right, inner, out):
@@ -131,27 +166,15 @@
 
 
 def advance_body(
-    downflow, shear, counts, cells, far_table, far_synth, far_fields, far_cells,
-    out, start, first, second, table, synth, sort_fields, sort_cells, done,
+    cells, flow_row, slope_row, mask, table, synth, sort_fields, sort_cells,
+    out, start, first, second,
 ):
-    fetch_table = pltpu.make_async_copy(far_table, table, done.at[0])
-    fetch_fields = pltpu.make_async_copy(far_fields, sort_fields, done.at[1])
-    fetch_cells = pltpu.make_async_copy(far_cells, sort_cells, done.at[2])
-    fetch_synth = pltpu.make_async_copy(far_synth, synth, done.at[3])
-    fetch_cells.start()
-    fetch_table.start()
-    fetch_fields.start()
-    fetch_synth.start()
     chunk = 64
     edge = 8
     lane = lanes_of(chunk)
     component = lane // STRIDE
-    plane = lane % STRIDE // SLOT
-    flow = jnp.zeros((chunk, LANES), jnp.float32)
-    slope = jnp.zeros((chunk, LANES), jnp.float32)
-    for p in range(PLANES):
-        flow = jnp.where(plane == p, downflow[p], flow)
-        slope = jnp.where((plane == p) & (component == 0), shear[p], slope)
+    flow = jnp.broadcast_to(flow_row[:1], (chunk, LANES))
+    slope = jnp.broadcast_to(slope_row[:1], (chunk, LANES))
 
     def store(ref, row, values):
         ref[edge + row : edge + row + chunk] = values
@@ -196,7 +219,6 @@
         begin = start[edge + row : edge + row + chunk]
         store(second, row, 0.75 * begin + 0.25 * (middle + time_step * change))
     in_eight = lax.broadcasted_iota(jnp.int32, (chunk, LANES), 0) % 8
-    fetch_cells.wait()
     part = (lane + LANES - 3) % LANES % SLOT // 4
     part = jnp.where((lane >= 3) & (lane < 127), part, 3)
     for row in rows:
@@ -214,18 +236,7 @@
         for block in range(chunk // 16):
             place = (row // 16 + block) * BACK + 16
             out[place : place + 2] = rest[2 * block : 2 * block + 2]
-    fetch_table.wait()
-    fetch_fields.wait()
-    coeffs = picked(table_dot(table[0], table[1], first[:NZ]), sort_fields[...])
-    mode = lax.broadcasted_iota(jnp.int32, (MODES, LANES), 0)
-    number = jnp.where(mode < HALF, mode, mode - HALF + 1)
-    plane = lanes_of(MODES) % PLANES
-    limit = jnp.zeros((MODES, LANES), jnp.int32)
-    for p in range(PLANES):
-        limit = jnp.where(plane == p, counts[1, p], limit)
-    weight = jnp.where(mode == 0, 1.0 / NZ, 2.0 / NZ)
-    coeffs = jnp.where(number <= limit, coeffs * weight, 0.0)
-    fetch_synth.wait()
+    coeffs = picked(table_dot(table[0], table[1], first[:NZ]), sort_fields[...]) * mask[...]
     filtered = table_dot(synth[0], synth[1], coeffs) + start[edge : edge + NZ]
     for block in range(GZ):
         out[block * BACK : block * BACK + 16] = filtered[16 * block : 16 * block + 16]
@@ -272,29 +283,14 @@
             out[c, p] = rows[pl.ds(c * PLANES + p, TILE_Z, stride=16), :]
 
 
-def streamwise_body(counts, lines, far_table, out, rows, table, done):
-    fetches = [
-        pltpu.make_async_copy(far_table.at[column], table.at[column], done.at[column])
-        for column in range(4)
-    ]
-    for fetch in fetches:
-        fetch.start()
+def streamwise_body(lines, mask, table, out, rows):
     cells = lines[...].reshape(NX // 4, LANES)
-    fetches[0].wait()
     coeffs = table_dot(table[0, 0], table[0, 1], cells)
     for column in range(1, 4):
-        fetches[column].wait()
         coeffs = coeffs + roll(
             table_dot(table[column, 0], table[column, 1], cells), -FIELDS * column, 1
         )
-    mode = lax.broadcasted_iota(jnp.int32, (MODES, LANES), 0)
-    number = jnp.where(mode < HALF, mode, mode - HALF + 1)
-    weight = jnp.where(mode == 0, 1.0 / NX, 2.0 / NX)
-    lane = lanes_of(MODES)
-    limit = jnp.full((MODES, LANES), -1, jnp.int32)
-    for p in range(PLANES):
-        limit = jnp.where((lane < FIELDS) & (lane % PLANES == p), counts[0, p], limit)
-    coeffs = jnp.where(number <= limit, coeffs * weight, 0.0).T[:32]
+    coeffs = jnp.where(lanes_of(MODES) < FIELDS, coeffs * mask[...], 0.0).T[:32]
     rows[...] = jnp.zeros(rows.shape, jnp.float32)
     for column in range(4):
         filtered = dot_table(coeffs, table[column, 0], table[column, 1])
@@ -374,14 +370,25 @@
     mode_counts = mode_counts.T
     left = lax.ppermute(velocity, "gx", [(i, (i + 1) % count) for i in range(count)])
     right = lax.ppermute(velocity, "gx", [((i + 1) % count, i) for i in range(count)])
-    analysis_z, synth_z, sort_fields, sort_cells, synth_x = wave_tables()
-    (inner,) = call(inner_body, [(GZ, TILE_Z, LANES)], 0, [], velocity)
+    tables = [velocity, *wave_tables()]
+    inner, flow, slope, mask_z, mask_x, *tables = call(
+        inner_body,
+        [(GZ, TILE_Z, LANES), (8, LANES), (8, LANES), (MODES, LANES), (MODES, LANES), *tables],
+        3,
+        [],
+        downflow,
+        shear,
+        mode_counts,
+        *tables,
+        tables=6,
+    )
+    own, analysis_z, synth_z, sort_fields, sort_cells, synth_x = tables
     (cells,) = call(
         outer_body,
         [(GZ, TILE_Z, LANES)],
         0,
         [],
-        velocity,
+        own,
         left,
         right,
         inner,
@@ -391,17 +398,16 @@
     (cells,) = call(
         advance_body,
         [(GZ * BACK, LANES)],
-        3,
+        0,
         [(NZ + 16, LANES)] * 3,
-        downflow,
-        shear,
-        mode_counts,
         cells,
+        flow,
+        slope,
+        mask_z,
         analysis_z,
         synth_z,
         sort_fields,
         sort_cells,
-        tables=4,
     )
     cells = exchange(cells, spanwise, GZ)
     (lines,) = call(forward_body, [(GX, GZ, LANES)], 0, [], cells)
@@ -412,12 +418,11 @@
     (lines,) = call(
         streamwise_body,
         [(GX * STRESSES, LANES)],
-        1,
+        0,
         [(4, 24, NX // 4)],
-        mode_counts,
         lines,
+        mask_x,
         synth_x,
-        tables=1,
     )
     lines = exchange(lines, "gx", GX)
     (stress,) = call(

time: 89.3 us -> 85.6 us (0.959)
  Pallas kernels: 11.2 us -> 9.31 us
  local copies, waits for them, and re-layouts: 0.92 us -> 0 us
    pallas_call x7, Pallas kernels: 11.2 us -> 9.31 us  [call(): pl.pallas_call(body, out_shape=[make(shape.shape, shape.dtype) if isinsta...]
    all_to_all x1, blocking collectives: 19.7 us -> 18.7 us  [local(): cells = lax.all_to_all(cells, spanwise, 0, 0, tiled=True)]
    unnamed x2 -> x0, local copies, waits for them, and re-layouts: 0.92 us -> none
  transfers between devices with their start and end apart: 3 -> 3, of which waited for: 2 -> 1; matrix products, arithmetic and copies ran while one was open for 0% -> 0% of each run, Pallas kernels for 2% -> 5%
where the time goes in v6:
time: 85.6 us; the launch traced here: 85.3 us
  blocking collectives  57.5 us (67%)
  starting transfers between devices  10.3 us (12%)
  Pallas kernels  9.31 us (11%)
  waiting for transfers between devices  7.59 us (9%)
    all_to_all x1, blocking collectives, local(): lines = lax.all_to_all(lines, 'gx', 0, 0, tiled=True)  24.5 us
    all_to_all x1, blocking collectives, local(): cells = lax.all_to_all(cells, spanwise, 0, 0, tiled=True)  18.7 us
    all_to_all x1, blocking collectives, exchange(): return lax.all_to_all(sent, axis, 0, 0, tiled=True).reshape(rows.shape)  14.3 us
    pallas_call x7, Pallas kernels, call(): pl.pallas_call(body, out_shape=[make(shape.shape, shape.dtype) if isinsta...  9.31 us
    all_to_all x1, waiting for transfers between devices, exchange(): return lax.all_to_all(sent, axis, 0, 0, tiled=True).reshape(rows.shape)  7.58 us
    ppermute x1, starting transfers between devices, local(): lax.ppermute(velocity, 'gx', [((i + 1) % count, i) for i in range(count)])  6.85 us
    all_to_all x1, starting transfers between devices, exchange(): return lax.all_to_all(sent, axis, 0, 0, tiled=True).reshape(rows.shape)  3.41 us
  transfers between devices with their start and end apart: 3, of which 1 were waited for; matrix products, arithmetic and copies ran while one was open for 0% of the time, Pallas kernels for 5%

profile of v6, /device:TPU:1, one launch (start us, length us, event | category | flops | bytes accessed | tf_op | source)
XLA Modules:
  0.0 85.3 jit_solution(8161612931101711915)
XLA Ops:
  0.6 6.9 %collective-permute-start.1 = (f32[3,3,16,128]{3,2,1,0:T(8,128)}, f32[3,3,16,128]{3,2,1,0:T(8,128)S(1)}, u32[]{:S(2)}, u32[]{:S(2)}) collective-permute-start(f32[3,3,16,128]{3,2,1,0:T(8,128)} %refs_0_.1), channel_id=1, source_target_pairs={{32,0},{64,32},{96,64},{128,96},{160,128},{192,160},{224,192},{256... | collective-permute-start | bytes 221192 | tf_op jit(solution)/shard_map/ppermute | solution.py:372
  7.5 0.0 collective-permute-start
  7.5 2.8 %shard_map.104 = (f32[32,16,128]{2,1,0:T(8,128)S(1)}, f32[8,128]{1,0:T(8,128)S(1)}, f32[8,128]{1,0:T(8,128)S(1)}, f32[256,128]{1,0:T(8,128)S(1)}, f32[256,128]{1...) custom-call(f32[3]{0:T(128)} %downflow.1, ...), custom_call_target="tpu_custom_call" | custom-call | tf_op jit(solution)/shard_map/pallas_call | solution.py:48
  10.2 0.0 collective-permute-done.1.right
  10.3 0.0 collective-permute-done.left
  10.3 0.1 shard_map.105
  10.4 18.7 %all_to_all.20.cells = f32[32,16,128]{2,1,0:T(8,128)S(1)} all-to-all(f32[32,16,128]{2,1,0:T(8,128)S(1)} %shard_map.105), channel_id=1, replica_groups=mesh['gx'=16,'gz'=16,'grp'=2] {'gz','grp'}, dimensions={0} | all-to-all | bytes 524288 | tf_op jit(solution)/shard_map/all_to_all | solution.py:397
  29.1 2.3 %shard_map.106 = f32[576,128]{1,0:T(8,128)S(1)} custom-call(f32[32,16,128]{2,1,0:T(8,128)S(1)} %all_to_all.20.cells, f32[8,128]{1,0:T(8,128)S(1)} %get-tuple-element.15.flow_row, f32[8,128]{1,0:T(8,128)S(1)} %get-tuple-element.16.slope_row, f32[256,128]{1,0:T(8,128)S(1)} %get-tuple-element.17.mask, bf16[2,256,512]{2,1,0:T(8,128)(2,1)S(1)} %get-tuple-element.18.table, ...), custom_call_target="tpu_custom_call" | custom-call | tf_op jit(solution)/shard_map/pallas_call | solution.py:48
  31.4 14.3 %all_to_all.21 = f32[32,9,2,128]{3,2,1,0:T(2,128)S(1)} all-to-all(f32[32,9,2,128]{3,2,1,0:T(2,128)S(1)} %bitcast.7), channel_id=1, replica_groups=mesh['gx'=16,'gz'=16,'grp'=2] {'gz','grp'}, dimensions={0} | all-to-all | bytes 589824 | tf_op jit(solution)/shard_map/all_to_all | solution.py:365
  45.7 24.5 %all_to_all.22.lines = f32[16,32,128]{2,1,0:T(8,128)S(1)} all-to-all(f32[16,32,128]{2,1,0:T(8,128)S(1)} %shard_map.108), channel_id=1, replica_groups=mesh['gx'=16,'gz'=16,'grp'=2] {'gx'}, dimensions={0} | all-to-all | bytes 524288 | tf_op jit(solution)/shard_map/all_to_all | solution.py:414
  70.2 2.0 %shard_map.109 = f32[288,128]{1,0:T(8,128)} custom-call(f32[16,32,128]{2,1,0:T(8,128)S(1)} %all_to_all.22.lines, f32[256,128]{1,0:T(8,128)S(1)} %get-tuple-element.22.mask, bf16[4,2,256,512]{3,2,1,0:T(8,128)(2,1)S(1)} %get-tuple-element.23.table), custom_call_target="tpu_custom_call" | custom-call | tf_op jit(solution)/shard_map/pallas_call | solution.py:48
  72.3 3.4 %all-to-all-start.3 = ((f32[16,9,2,128]{3,2,1,0:T(2,128)}), f32[16,9,2,128]{3,2,1,0:T(2,128)S(1)}, u32[]{:S(2)}, u32[]{:S(2)}) async-start(f32[16,9,2,128]{3,2,1,0:T(2,128)} %bitcast.3), calls=%async_computation.3 | async-start | bytes 294912 | tf_op jit(solution)/shard_map/all_to_all | solution.py:365
  75.7 1.2 %shard_map.107 = f32[3,3,16,128]{3,2,1,0:T(8,128)} custom-call(f32[576,128]{1,0:T(8,128)S(1)} %bitcast.6), custom_call_target="tpu_custom_call" | custom-call | tf_op jit(solution)/shard_map/pallas_call | solution.py:48
  76.8 7.6 %all-to-all-done.3 = f32[16,9,2,128]{3,2,1,0:T(2,128)S(1)} async-done(((f32[16,9,2,128]{3,2,1,0:T(2,128)}), f32[16,9,2,128]{3,2,1,0:T(2,128)S(1)}, u32[]{:S(2)}, u32[]{:S(2)}) %all-to-all-start.3) | async-done | bytes 147488 | tf_op jit(solution)/shard_map/all_to_all | solution.py:365
  84.4 0.9 %shard_map.110 = f32[6,3,16,128]{3,2,1,0:T(8,128)} custom-call(f32[288,128]{1,0:T(8,128)S(1)} %bitcast.8), custom_call_target="tpu_custom_call" | custom-call | tf_op jit(solution)/shard_map/pallas_call | solution.py:48
  (1 shorter events, 0.0 us)
Async XLA Ops:
  0.6 9.6 %collective-permute-start.1 = (f32[3,3,16,128]{3,2,1,0:T(8,128)}, f32[3,3,16,128]{3,2,1,0:T(8,128)S(1)}, u32[]{:S(2)}, u32[]{:S(2)}) collective-permute-start(f32[3,3,16,128]{3,2,1,0:T(8,128)} %refs_0_.1), channel_id=1, source_target_pairs={{32,0},{64,32},{96,64},{128,96},{160,128},{192,160},{224,192},{256... | collective-permute-start | bytes 221192 | tf_op jit(solution)/shard_map/ppermute | solution.py:372
  7.5 2.8 %collective-permute-start = (f32[3,3,16,128]{3,2,1,0:T(8,128)}, f32[3,3,16,128]{3,2,1,0:T(8,128)S(1)}, u32[]{:S(2)}, u32[]{:S(2)}) collective-permute-start(f32[3,3,16,128]{3,2,1,0:T(8,128)} %refs_0_.1), channel_id=1, source_target_pairs={{0,32},{32,64},{64,96},{96,128},{128,160},{160,192},{192,224},{224... | collective-permute-start | bytes 221192 | tf_op jit(solution)/shard_map/ppermute | solution.py:371
  72.3 12.2 %all-to-all-start.3 = ((f32[16,9,2,128]{3,2,1,0:T(2,128)}), f32[16,9,2,128]{3,2,1,0:T(2,128)S(1)}, u32[]{:S(2)}, u32[]{:S(2)}) async-start(f32[16,9,2,128]{3,2,1,0:T(2,128)} %bitcast.3), calls=%async_computation.3 | async-start | bytes 294912 | tf_op jit(solution)/shard_map/all_to_all | solution.py:365

commit v7 on v6

--- a/solution.py
+++ b/solution.py
@@ -23,6 +23,7 @@
 STRIDE = PLANES * SLOT
 FIELDS = 9 * PLANES
 BACK = 18
+SENT = 12
 STRESSES = 6 * PLANES
 
 molecular_diffusivity = 0.4
@@ -107,14 +108,18 @@
     return lax.broadcasted_iota(jnp.int32, (rows, LANES), 1)
 
 
-def packed_for(dest, sides):
+def pack_for(out, dest, sides):
     lane = lanes_of(TILE_Z)
     packed = jnp.zeros((TILE_Z, LANES), jnp.float32)
     for index, values in enumerate(sides):
         moved = roll(values, index * SLOT - (4 * dest - 3), 1)
         here = (lane >= index * SLOT) & (lane < index * SLOT + 10)
         packed = jnp.where(here, moved, packed)
-    return packed
+    own_lane = lanes_of(4) % SLOT < 10
+    for part in range(3):
+        rest = roll(packed[SENT:], 10 - 4 * part, 1)
+        place = dest * SENT + 4 * part
+        out[place : place + 4] = jnp.where(own_lane, packed[4 * part : 4 * part + 4], rest)
 
 
 def inner_body(downflow, shear, counts, *refs):
@@ -131,9 +136,7 @@
     fetches[0].wait()
     cells = [near[0][c, p] for c in range(3) for p in range(PLANES)]
     for dest in range(1, GZ - 1):
-        out[dest] = packed_for(dest, cells)
-    out[0] = packed_for(GZ // 2, cells)
-    out[GZ - 1] = packed_for(GZ // 2, cells)
+        pack_for(out, dest, cells)
     lane = lanes_of(8)
     plane = lane % STRIDE // SLOT
     speeds = jnp.zeros((8, LANES), jnp.float32)
@@ -159,10 +162,8 @@
 def outer_body(own, left, right, inner, out):
     low = lanes_of(TILE_Z) < LANES // 2
     pairs = [(c, p) for c in range(3) for p in range(PLANES)]
-    out[0] = packed_for(0, [jnp.where(low, own[c, p], left[c, p]) for c, p in pairs])
-    out[GZ - 1] = packed_for(
-        GZ - 1, [jnp.where(low, right[c, p], own[c, p]) for c, p in pairs]
-    )
+    pack_for(out, 0, [jnp.where(low, own[c, p], left[c, p]) for c, p in pairs])
+    pack_for(out, GZ - 1, [jnp.where(low, right[c, p], own[c, p]) for c, p in pairs])
 
 
 def advance_body(
@@ -209,8 +210,17 @@
         )
 
     rows = range(0, NZ, chunk)
-    for row in rows:
-        store(start, row, cells[row // 16 : (row + chunk) // 16].reshape(chunk, LANES))
+    column = lanes_of(4) % SLOT
+    for block in range(GZ):
+        rest = jnp.zeros((4, LANES), jnp.float32)
+        place = edge + block * 16
+        for index in range(3):
+            piece = cells[block * SENT + 4 * index : block * SENT + 4 * index + 4]
+            start[place + 4 * index : place + 4 * index + 4] = piece
+            rest = jnp.where(column // 4 == index, roll(piece, 4 * index - 10, 1), rest)
+        start[place + SENT : place + 16] = rest
+    start[:edge] = start[NZ : NZ + edge]
+    start[edge + NZ :] = start[edge : 2 * edge]
     for row in rows:
         middle, change = rate(start, row)
         store(first, row, middle + time_step * change)
@@ -373,7 +383,7 @@
     tables = [velocity, *wave_tables()]
     inner, flow, slope, mask_z, mask_x, *tables = call(
         inner_body,
-        [(GZ, TILE_Z, LANES), (8, LANES), (8, LANES), (MODES, LANES), (MODES, LANES), *tables],
+        [(GZ * SENT, LANES), (8, LANES), (8, LANES), (MODES, LANES), (MODES, LANES), *tables],
         3,
         [],
         downflow,
@@ -385,7 +395,7 @@
     own, analysis_z, synth_z, sort_fields, sort_cells, synth_x = tables
     (cells,) = call(
         outer_body,
-        [(GZ, TILE_Z, LANES)],
+        [(GZ * SENT, LANES)],
         0,
         [],
         own,
@@ -394,7 +404,7 @@
         inner,
         alias={3: 0},
     )
-    cells = lax.all_to_all(cells, spanwise, 0, 0, tiled=True)
+    cells = exchange(cells, spanwise, GZ)
     (cells,) = call(
         advance_body,
         [(GZ * BACK, LANES)],

time: 85.6 us -> 86.3 us (level)
  Pallas kernels: 9.31 us -> 10.8 us
    all_to_all x1 -> x0, blocking collectives: 18.7 us -> none  [local(): cells = lax.all_to_all(cells, spanwise, 0, 0, tiled=True)]
    all_to_all x1 -> x2, blocking collectives: 14.3 us -> 32.3 us  [exchange(): return lax.all_to_all(sent, axis, 0, 0, tiled=True).reshape(rows.shape)]
    pallas_call x7, Pallas kernels: 9.31 us -> 10.8 us  [call(): pl.pallas_call(body, out_shape=[make(shape.shape, shape.dtype) if isinsta...]
  transfers between devices with their start and end apart: 3 -> 3, of which waited for: 1 -> 1; matrix products, arithmetic and copies ran while one was open for 0% -> 0% of each run, Pallas kernels for 5% -> 6%
where the time goes in v7:
time: 86.3 us; the launch traced here: 86 us
  blocking collectives  56.7 us (66%)
  Pallas kernels  10.8 us (13%)
  starting transfers between devices  10.3 us (12%)
  waiting for transfers between devices  7.58 us (9%)
    all_to_all x2, blocking collectives, exchange(): return lax.all_to_all(sent, axis, 0, 0, tiled=True).reshape(rows.shape)  32.3 us
    all_to_all x1, blocking collectives, local(): lines = lax.all_to_all(lines, 'gx', 0, 0, tiled=True)  24.4 us
    pallas_call x7, Pallas kernels, call(): pl.pallas_call(body, out_shape=[make(shape.shape, shape.dtype) if isinsta...  10.8 us
    all_to_all x1, waiting for transfers between devices, exchange(): return lax.all_to_all(sent, axis, 0, 0, tiled=True).reshape(rows.shape)  7.58 us
    ppermute x1, starting transfers between devices, local(): lax.ppermute(velocity, 'gx', [((i + 1) % count, i) for i in range(count)])  6.85 us
    all_to_all x1, starting transfers between devices, exchange(): return lax.all_to_all(sent, axis, 0, 0, tiled=True).reshape(rows.shape)  3.41 us
  transfers between devices with their start and end apart: 3, of which 1 were waited for; matrix products, arithmetic and copies ran while one was open for 0% of the time, Pallas kernels for 6%

profile of v7, /device:TPU:1, one launch (start us, length us, event | category | flops | bytes accessed | tf_op | source)
XLA Modules:
  0.0 86.0 jit_solution(11593818942230817955)
XLA Ops:
  0.6 6.9 %collective-permute-start.1 = (f32[3,3,16,128]{3,2,1,0:T(8,128)}, f32[3,3,16,128]{3,2,1,0:T(8,128)S(1)}, u32[]{:S(2)}, u32[]{:S(2)}) collective-permute-start(f32[3,3,16,128]{3,2,1,0:T(8,128)} %refs_0_.1), channel_id=1, source_target_pairs={{32,0},{64,32},{96,64},{128,96},{160,128},{192,160},{224,192},{256... | collective-permute-start | bytes 221192 | tf_op jit(solution)/shard_map/ppermute | solution.py:382
  7.5 0.0 collective-permute-start
  7.5 4.1 %shard_map.104 = (f32[384,128]{1,0:T(8,128)S(1)}, f32[8,128]{1,0:T(8,128)S(1)}, f32[8,128]{1,0:T(8,128)S(1)}, f32[256,128]{1,0:T(8,128)S(1)}, f32[256,128]{1,0:T...) custom-call(f32[3]{0:T(128)} %downflow.1, ...), custom_call_target="tpu_custom_call" | custom-call | tf_op jit(solution)/shard_map/pallas_call | solution.py:49
  11.6 0.0 collective-permute-done.1.right
  11.6 0.0 collective-permute-done.left
  11.6 0.2 shard_map.105
  11.7 18.3 %all_to_all.20 = f32[32,6,2,128]{3,2,1,0:T(2,128)S(1)} all-to-all(f32[32,6,2,128]{3,2,1,0:T(2,128)S(1)} %bitcast.11), channel_id=1, replica_groups=mesh['gx'=16,'gz'=16,'grp'=2] {'gz','grp'}, dimensions={0} | all-to-all | bytes 393216 | tf_op jit(solution)/shard_map/all_to_all | solution.py:375
  30.1 2.4 %shard_map.106 = f32[576,128]{1,0:T(8,128)S(1)} custom-call(f32[384,128]{1,0:T(8,128)S(1)} %bitcast.10, f32[8,128]{1,0:T(8,128)S(1)} %get-tuple-element.15.flow_row, f32[8,128]{1,0:T(8,128)S(1)} %get-tuple-element.16.slope_row, f32[256,128]{1,0:T(8,128)S(1)} %get-tuple-element.17.mask, bf16[2,256,512]{2,1,0:T(8,128)(2,1)S(1)} %get-tuple-element.18.table, ...), custom_call_target="tpu_custom_call" | custom-call | tf_op jit(solution)/shard_map/pallas_call | solution.py:49
  32.5 13.9 %all_to_all.21 = f32[32,9,2,128]{3,2,1,0:T(2,128)S(1)} all-to-all(f32[32,9,2,128]{3,2,1,0:T(2,128)S(1)} %bitcast.9), channel_id=1, replica_groups=mesh['gx'=16,'gz'=16,'grp'=2] {'gz','grp'}, dimensions={0} | all-to-all | bytes 589824 | tf_op jit(solution)/shard_map/all_to_all | solution.py:375
  46.5 24.4 %all_to_all.22.lines = f32[16,32,128]{2,1,0:T(8,128)S(1)} all-to-all(f32[16,32,128]{2,1,0:T(8,128)S(1)} %shard_map.108), channel_id=1, replica_groups=mesh['gx'=16,'gz'=16,'grp'=2] {'gx'}, dimensions={0} | all-to-all | bytes 524288 | tf_op jit(solution)/shard_map/all_to_all | solution.py:424
  70.9 2.0 %shard_map.109 = f32[288,128]{1,0:T(8,128)} custom-call(f32[16,32,128]{2,1,0:T(8,128)S(1)} %all_to_all.22.lines, f32[256,128]{1,0:T(8,128)S(1)} %get-tuple-element.22.mask, bf16[4,2,256,512]{3,2,1,0:T(8,128)(2,1)S(1)} %get-tuple-element.23.table), custom_call_target="tpu_custom_call" | custom-call | tf_op jit(solution)/shard_map/pallas_call | solution.py:49
  72.9 3.4 %all-to-all-start.3 = ((f32[16,9,2,128]{3,2,1,0:T(2,128)}), f32[16,9,2,128]{3,2,1,0:T(2,128)S(1)}, u32[]{:S(2)}, u32[]{:S(2)}) async-start(f32[16,9,2,128]{3,2,1,0:T(2,128)} %bitcast.5), calls=%async_computation.3 | async-start | bytes 294912 | tf_op jit(solution)/shard_map/all_to_all | solution.py:375
  76.4 1.2 %shard_map.107 = f32[3,3,16,128]{3,2,1,0:T(8,128)} custom-call(f32[576,128]{1,0:T(8,128)S(1)} %bitcast.8), custom_call_target="tpu_custom_call" | custom-call | tf_op jit(solution)/shard_map/pallas_call | solution.py:49
  77.5 7.6 %all-to-all-done.3 = f32[16,9,2,128]{3,2,1,0:T(2,128)S(1)} async-done(((f32[16,9,2,128]{3,2,1,0:T(2,128)}), f32[16,9,2,128]{3,2,1,0:T(2,128)S(1)}, u32[]{:S(2)}, u32[]{:S(2)}) %all-to-all-start.3) | async-done | bytes 147488 | tf_op jit(solution)/shard_map/all_to_all | solution.py:375
  85.1 0.9 %shard_map.110 = f32[6,3,16,128]{3,2,1,0:T(8,128)} custom-call(f32[288,128]{1,0:T(8,128)S(1)} %bitcast.12), custom_call_target="tpu_custom_call" | custom-call | tf_op jit(solution)/shard_map/pallas_call | solution.py:49
  (1 shorter events, 0.0 us)
Async XLA Ops:
  0.6 10.9 %collective-permute-start.1 = (f32[3,3,16,128]{3,2,1,0:T(8,128)}, f32[3,3,16,128]{3,2,1,0:T(8,128)S(1)}, u32[]{:S(2)}, u32[]{:S(2)}) collective-permute-start(f32[3,3,16,128]{3,2,1,0:T(8,128)} %refs_0_.1), channel_id=1, source_target_pairs={{32,0},{64,32},{96,64},{128,96},{160,128},{192,160},{224,192},{256... | collective-permute-start | bytes 221192 | tf_op jit(solution)/shard_map/ppermute | solution.py:382
  7.5 4.1 %collective-permute-start = (f32[3,3,16,128]{3,2,1,0:T(8,128)}, f32[3,3,16,128]{3,2,1,0:T(8,128)S(1)}, u32[]{:S(2)}, u32[]{:S(2)}) collective-permute-start(f32[3,3,16,128]{3,2,1,0:T(8,128)} %refs_0_.1), channel_id=1, source_target_pairs={{0,32},{32,64},{64,96},{96,128},{128,160},{160,192},{192,224},{224... | collective-permute-start | bytes 221192 | tf_op jit(solution)/shard_map/ppermute | solution.py:381
  72.9 12.2 %all-to-all-start.3 = ((f32[16,9,2,128]{3,2,1,0:T(2,128)}), f32[16,9,2,128]{3,2,1,0:T(2,128)S(1)}, u32[]{:S(2)}, u32[]{:S(2)}) async-start(f32[16,9,2,128]{3,2,1,0:T(2,128)} %bitcast.5), calls=%async_computation.3 | async-start | bytes 294912 | tf_op jit(solution)/shard_map/all_to_all | solution.py:375

commit v8 on v7

--- a/solution.py
+++ b/solution.py
@@ -38,7 +38,7 @@
     return pltpu.roll(values, shift, axis) if shift else values
 
 
-def call(body, out_shapes, smem, scratch, *args, tables=0, final=False, alias=None):
+def call(body, out_shapes, smem, scratch, *args, tables=0, final=False, alias=None, extra=()):
     make = jax.ShapeDtypeStruct if final else pltpu.VMEM
     near = len(args) - tables
     args = (
@@ -59,6 +59,7 @@
         + [pl.BlockSpec(memory_space=pltpu.HBM)] * tables,
         out_specs=[pl.BlockSpec(memory_space=pltpu.VMEM)] * len(out_shapes),
         scratch_shapes=[pltpu.VMEM(shape, jnp.float32) for shape in scratch]
+        + list(extra)
         + ([pltpu.SemaphoreType.DMA((tables,))] if tables else []),
         compiler_params=pltpu.CompilerParams(vmem_limit_bytes=16 << 20),
         input_output_aliases=alias or {},
@@ -115,18 +116,22 @@
         moved = roll(values, index * SLOT - (4 * dest - 3), 1)
         here = (lane >= index * SLOT) & (lane < index * SLOT + 10)
         packed = jnp.where(here, moved, packed)
-    own_lane = lanes_of(4) % SLOT < 10
-    for part in range(3):
-        rest = roll(packed[SENT:], 10 - 4 * part, 1)
-        place = dest * SENT + 4 * part
-        out[place : place + 4] = jnp.where(own_lane, packed[4 * part : 4 * part + 4], rest)
-
-
-def inner_body(downflow, shear, counts, *refs):
-    far = refs[:6]
-    out, flow, slope, mask_z, mask_x = refs[6:11]
-    near = refs[11:17]
-    done = refs[17]
+    own_lane = lanes_of(8) % SLOT < 10
+    low = lax.broadcasted_iota(jnp.int32, (8, LANES), 0) < 4
+    last = packed[8:]
+    turned = roll(last, 4, 0)
+    rest = jnp.where(low, roll(turned, 10, 1), roll(last, 6, 1))
+    place = dest * SENT
+    out[place : place + 8] = jnp.where(own_lane, packed[:8], rest)
+    out[place + 8 : place + SENT] = jnp.where(own_lane, last, roll(turned, 2, 1))[:4]
+
+
+def inner_body(*refs):
+    far = refs[:9]
+    out, flow, slope, mask_z, mask_x = refs[9:14]
+    near = refs[14:23]
+    downflow, shear, counts = refs[20:23]
+    done = refs[23]
     fetches = [
         pltpu.make_async_copy(source, target, done.at[index])
         for index, (source, target) in enumerate(zip(far, near))
@@ -137,6 +142,8 @@
     cells = [near[0][c, p] for c in range(3) for p in range(PLANES)]
     for dest in range(1, GZ - 1):
         pack_for(out, dest, cells)
+    for fetch in fetches[6:]:
+        fetch.wait()
     lane = lanes_of(8)
     plane = lane % STRIDE // SLOT
     speeds = jnp.zeros((8, LANES), jnp.float32)
@@ -155,7 +162,7 @@
             limit = jnp.where(plane == p, counts[axis, p], limit)
         weight = jnp.where(mode == 0, 1.0 / length, 2.0 / length)
         mask[...] = jnp.where(number <= limit, weight, 0.0)
-    for fetch in fetches[1:]:
+    for fetch in fetches[1:6]:
         fetch.wait()
 
 
@@ -228,7 +235,6 @@
         middle, change = rate(first, row)
         begin = start[edge + row : edge + row + chunk]
         store(second, row, 0.75 * begin + 0.25 * (middle + time_step * change))
-    in_eight = lax.broadcasted_iota(jnp.int32, (chunk, LANES), 0) % 8
     part = (lane + LANES - 3) % LANES % SLOT // 4
     part = jnp.where((lane >= 3) & (lane < 127), part, 3)
     for row in rows:
@@ -240,8 +246,9 @@
         fields = jnp.where(part == 1, roll(last * last, 4, 1), fields)
         first[row : row + chunk] = jnp.where(part == 2, roll(last * other, 8, 1), fields)
         sorted_cells = picked(jnp.where(part == 0, last, 0.0), sort_cells[...])
-        start[edge + row : edge + row + chunk] = sorted_cells[:, :LANES]
-        rest = jnp.where(lane // 16 == in_eight, sorted_cells[:, LANES:], 0.0)
+        start[edge + row : edge + row + chunk] = jnp.where(lane < 16, 0.0, sorted_cells)
+        rest = jnp.where(lane < 16, sorted_cells, 0.0)
+        rest = pltpu.roll(rest, 0, 1, stride=16, stride_axis=0)
         rest = jnp.sum(rest.reshape(chunk // 8, 8, LANES), axis=1)
         for block in range(chunk // 16):
             place = (row // 16 + block) * BACK + 16
@@ -337,7 +344,7 @@
     synth_z = wave_table(NZ).T
     synth_x = wave_table(NX).reshape(NX // 4, 4, MODES).transpose(1, 2, 0)
     sort_fields = np.zeros((LANES, LANES))
-    sort_cells = np.zeros((LANES, 2 * LANES))
+    sort_cells = np.zeros((LANES, LANES))
     kinds = ((0, 1, 2), (3, 6, 8), (4, 7, 5))
     for c in range(3):
         for p in range(PLANES):
@@ -350,8 +357,7 @@
                 if index < 5:
                     sort_cells[lane, 4 * FIELDS + column * 5 + index] = 1.0
                 else:
-                    begin = LANES + column * 4 + index - 5
-                    sort_cells[lane, begin : 2 * LANES : 16] = 1.0
+                    sort_cells[lane, column * 4 + index - 5] = 1.0
 
     def halves(values):
         high = values.astype(jnp.bfloat16)
@@ -384,13 +390,18 @@
     inner, flow, slope, mask_z, mask_x, *tables = call(
         inner_body,
         [(GZ * SENT, LANES), (8, LANES), (8, LANES), (MODES, LANES), (MODES, LANES), *tables],
-        3,
+        0,
         [],
+        *tables,
         downflow,
         shear,
         mode_counts,
-        *tables,
-        tables=6,
+        tables=9,
+        extra=[
+            pltpu.SMEM((PLANES,), jnp.float32),
+            pltpu.SMEM((PLANES,), jnp.float32),
+            pltpu.SMEM((2, PLANES), jnp.int32),
+        ],
     )
     own, analysis_z, synth_z, sort_fields, sort_cells, synth_x = tables
     (cells,) = call(

time: 86.3 us -> 85.3 us (0.988)
  transfers between devices with their start and end apart: 3 -> 3, of which waited for: 1 -> 1; matrix products, arithmetic and copies ran while one was open for 0% -> 0% of each run, Pallas kernels for 6% -> 5%
where the time goes in v8:
time: 85.3 us; the launch traced here: 85 us
  blocking collectives  56.3 us (66%)
  starting transfers between devices  10.3 us (12%)
  Pallas kernels  10.1 us (12%)
  waiting for transfers between devices  7.58 us (9%)
    all_to_all x2, blocking collectives, exchange(): return lax.all_to_all(sent, axis, 0, 0, tiled=True).reshape(rows.shape)  32.3 us
    all_to_all x1, blocking collectives, local(): lines = lax.all_to_all(lines, 'gx', 0, 0, tiled=True)  24 us
    pallas_call x7, Pallas kernels, call(): pl.pallas_call(body, out_shape=[make(shape.shape, shape.dtype) if isinsta...  10.1 us
    all_to_all x1, waiting for transfers between devices, exchange(): return lax.all_to_all(sent, axis, 0, 0, tiled=True).reshape(rows.shape)  7.57 us
    ppermute x1, starting transfers between devices, local(): lax.ppermute(velocity, 'gx', [((i + 1) % count, i) for i in range(count)])  6.85 us
    all_to_all x1, starting transfers between devices, exchange(): return lax.all_to_all(sent, axis, 0, 0, tiled=True).reshape(rows.shape)  3.41 us
  transfers between devices with their start and end apart: 3, of which 1 were waited for; matrix products, arithmetic and copies ran while one was open for 0% of the time, Pallas kernels for 5%

profile of v8, /device:TPU:1, one launch (start us, length us, event | category | flops | bytes accessed | tf_op | source)
XLA Modules:
  0.0 85.0 jit_solution(14218257409795350653)
XLA Ops:
  0.6 6.9 %collective-permute-start.1 = (f32[3,3,16,128]{3,2,1,0:T(8,128)}, f32[3,3,16,128]{3,2,1,0:T(8,128)S(1)}, u32[]{:S(2)}, u32[]{:S(2)}) collective-permute-start(f32[3,3,16,128]{3,2,1,0:T(8,128)} %refs_0_.1), channel_id=1, source_target_pairs={{32,0},{64,32},{96,64},{128,96},{160,128},{192,160},{224,192},{256... | collective-permute-start | bytes 221192 | tf_op jit(solution)/shard_map/ppermute | solution.py:388
  7.5 0.0 collective-permute-start
  7.5 3.5 %shard_map.104 = (f32[384,128]{1,0:T(8,128)S(1)}, f32[8,128]{1,0:T(8,128)S(1)}, f32[8,128]{1,0:T(8,128)S(1)}, f32[256,128]{1,0:T(8,128)S(1)}, f32[256,128]{1,0:T...) custom-call(f32[3,3,16,128]{3,2,1,0:T(8,128)} %refs_0_.1, ...), custom_call_target="tpu_custom_call" | custom-call | tf_op jit(solution)/shard_map/pallas_call | solution.py:49
  11.0 0.0 collective-permute-done.1.right
  11.0 0.0 collective-permute-done.left
  11.0 0.2 shard_map.105
  11.1 18.3 %all_to_all.20 = f32[32,6,2,128]{3,2,1,0:T(2,128)S(1)} all-to-all(f32[32,6,2,128]{3,2,1,0:T(2,128)S(1)} %bitcast.10), channel_id=1, replica_groups=mesh['gx'=16,'gz'=16,'grp'=2] {'gz','grp'}, dimensions={0} | all-to-all | bytes 393216 | tf_op jit(solution)/shard_map/all_to_all | solution.py:381
  29.4 2.4 %shard_map.106 = f32[576,128]{1,0:T(8,128)S(1)} custom-call(f32[384,128]{1,0:T(8,128)S(1)} %bitcast.11, f32[8,128]{1,0:T(8,128)S(1)} %get-tuple-element.15.flow_row, f32[8,128]{1,0:T(8,128)S(1)} %get-tuple-element.16.slope_row, f32[256,128]{1,0:T(8,128)S(1)} %get-tuple-element.17.mask, bf16[2,256,512]{2,1,0:T(8,128)(2,1)S(1)} %get-tuple-element.18.table, ...), custom_call_target="tpu_custom_call" | custom-call | tf_op jit(solution)/shard_map/pallas_call | solution.py:49
  31.9 14.0 %all_to_all.21 = f32[32,9,2,128]{3,2,1,0:T(2,128)S(1)} all-to-all(f32[32,9,2,128]{3,2,1,0:T(2,128)S(1)} %bitcast.9), channel_id=1, replica_groups=mesh['gx'=16,'gz'=16,'grp'=2] {'gz','grp'}, dimensions={0} | all-to-all | bytes 589824 | tf_op jit(solution)/shard_map/all_to_all | solution.py:381
  45.9 24.0 %all_to_all.22.lines = f32[16,32,128]{2,1,0:T(8,128)S(1)} all-to-all(f32[16,32,128]{2,1,0:T(8,128)S(1)} %shard_map.108), channel_id=1, replica_groups=mesh['gx'=16,'gz'=16,'grp'=2] {'gx'}, dimensions={0} | all-to-all | bytes 524288 | tf_op jit(solution)/shard_map/all_to_all | solution.py:435
  69.9 2.0 %shard_map.109 = f32[288,128]{1,0:T(8,128)} custom-call(f32[16,32,128]{2,1,0:T(8,128)S(1)} %all_to_all.22.lines, f32[256,128]{1,0:T(8,128)S(1)} %get-tuple-element.22.mask, bf16[4,2,256,512]{3,2,1,0:T(8,128)(2,1)S(1)} %get-tuple-element.23.table), custom_call_target="tpu_custom_call" | custom-call | tf_op jit(solution)/shard_map/pallas_call | solution.py:49
  71.9 3.4 %all-to-all-start.3 = ((f32[16,9,2,128]{3,2,1,0:T(2,128)}), f32[16,9,2,128]{3,2,1,0:T(2,128)S(1)}, u32[]{:S(2)}, u32[]{:S(2)}) async-start(f32[16,9,2,128]{3,2,1,0:T(2,128)} %bitcast.5), calls=%async_computation.3 | async-start | bytes 294912 | tf_op jit(solution)/shard_map/all_to_all | solution.py:381
  75.4 1.2 %shard_map.107 = f32[3,3,16,128]{3,2,1,0:T(8,128)} custom-call(f32[576,128]{1,0:T(8,128)S(1)} %bitcast.8), custom_call_target="tpu_custom_call" | custom-call | tf_op jit(solution)/shard_map/pallas_call | solution.py:49
  76.5 7.6 %all-to-all-done.3 = f32[16,9,2,128]{3,2,1,0:T(2,128)S(1)} async-done(((f32[16,9,2,128]{3,2,1,0:T(2,128)}), f32[16,9,2,128]{3,2,1,0:T(2,128)S(1)}, u32[]{:S(2)}, u32[]{:S(2)}) %all-to-all-start.3) | async-done | bytes 147488 | tf_op jit(solution)/shard_map/all_to_all | solution.py:381
  84.1 0.9 %shard_map.110 = f32[6,3,16,128]{3,2,1,0:T(8,128)} custom-call(f32[288,128]{1,0:T(8,128)S(1)} %bitcast.12), custom_call_target="tpu_custom_call" | custom-call | tf_op jit(solution)/shard_map/pallas_call | solution.py:49
  (1 shorter events, 0.0 us)
Async XLA Ops:
  0.6 10.3 %collective-permute-start.1 = (f32[3,3,16,128]{3,2,1,0:T(8,128)}, f32[3,3,16,128]{3,2,1,0:T(8,128)S(1)}, u32[]{:S(2)}, u32[]{:S(2)}) collective-permute-start(f32[3,3,16,128]{3,2,1,0:T(8,128)} %refs_0_.1), channel_id=1, source_target_pairs={{32,0},{64,32},{96,64},{128,96},{160,128},{192,160},{224,192},{256... | collective-permute-start | bytes 221192 | tf_op jit(solution)/shard_map/ppermute | solution.py:388
  7.5 3.5 %collective-permute-start = (f32[3,3,16,128]{3,2,1,0:T(8,128)}, f32[3,3,16,128]{3,2,1,0:T(8,128)S(1)}, u32[]{:S(2)}, u32[]{:S(2)}) collective-permute-start(f32[3,3,16,128]{3,2,1,0:T(8,128)} %refs_0_.1), channel_id=1, source_target_pairs={{0,32},{32,64},{64,96},{96,128},{128,160},{160,192},{192,224},{224... | collective-permute-start | bytes 221192 | tf_op jit(solution)/shard_map/ppermute | solution.py:387
  71.9 12.2 %all-to-all-start.3 = ((f32[16,9,2,128]{3,2,1,0:T(2,128)}), f32[16,9,2,128]{3,2,1,0:T(2,128)S(1)}, u32[]{:S(2)}, u32[]{:S(2)}) async-start(f32[16,9,2,128]{3,2,1,0:T(2,128)} %bitcast.5), calls=%async_computation.3 | async-start | bytes 294912 | tf_op jit(solution)/shard_map/all_to_all | solution.py:381

commit v9 on v8

--- a/solution.py
+++ b/solution.py
@@ -432,10 +432,11 @@
     )
     cells = exchange(cells, spanwise, GZ)
     (lines,) = call(forward_body, [(GX, GZ, LANES)], 0, [], cells)
-    lines = lax.all_to_all(lines, "gx", 0, 0, tiled=True)
     (advanced,) = call(
         cells_body, [(3, PLANES, TILE_Z, TILE_X)], 0, [(16 * TILE_Z, LANES)], cells, final=True
     )
+    lines, advanced = lax.optimization_barrier((lines, advanced))
+    lines = lax.all_to_all(lines, "gx", 0, 0, tiled=True)
     (lines,) = call(
         streamwise_body,
         [(GX * STRESSES, LANES)],

time: 85.3 us -> 85.6 us (level)
  blocking collectives: 56.3 us -> 68.3 us
  waiting for transfers between devices: 7.58 us -> 0.01 us
  starting transfers between devices: 10.3 us -> 6.85 us
    all_to_all x2 -> x3, blocking collectives: 32.3 us -> 44.3 us  [exchange(): return lax.all_to_all(sent, axis, 0, 0, tiled=True).reshape(rows.shape)]
    all_to_all x1 -> x0, waiting for transfers between devices: 7.57 us -> none  [exchange(): return lax.all_to_all(sent, axis, 0, 0, tiled=True).reshape(rows.shape)]
    all_to_all x1 -> x0, starting transfers between devices: 3.41 us -> none  [exchange(): return lax.all_to_all(sent, axis, 0, 0, tiled=True).reshape(rows.shape)]
  transfers between devices with their start and end apart: 3 -> 2, of which waited for: 1 -> 0; matrix products, arithmetic and copies ran while one was open for 0% -> 0% of each run, Pallas kernels for 5% -> 4%
where the time goes in v9:
time: 85.6 us; the launch traced here: 85.3 us
  blocking collectives  68.3 us (80%)
  Pallas kernels  9.48 us (11%)
  starting transfers between devices  6.85 us (8%)
    all_to_all x3, blocking collectives, exchange(): return lax.all_to_all(sent, axis, 0, 0, tiled=True).reshape(rows.shape)  44.3 us
    all_to_all x1, blocking collectives, local(): lines = lax.all_to_all(lines, 'gx', 0, 0, tiled=True)  24 us
    pallas_call x7, Pallas kernels, call(): pl.pallas_call(body, out_shape=[make(shape.shape, shape.dtype) if isinsta...  9.48 us
    ppermute x1, starting transfers between devices, local(): lax.ppermute(velocity, 'gx', [((i + 1) % count, i) for i in range(count)])  6.85 us
  transfers between devices with their start and end apart: 2, of which 0 were waited for; matrix products, arithmetic and copies ran while one was open for 0% of the time, Pallas kernels for 4%

profile of v9, /device:TPU:1, one launch (start us, length us, event | category | flops | bytes accessed | tf_op | source)
XLA Modules:
  0.0 85.3 jit_solution(16343839109552960565)
XLA Ops:
  0.6 6.9 %collective-permute-start.1 = (f32[3,3,16,128]{3,2,1,0:T(8,128)}, f32[3,3,16,128]{3,2,1,0:T(8,128)S(1)}, u32[]{:S(2)}, u32[]{:S(2)}) collective-permute-start(f32[3,3,16,128]{3,2,1,0:T(8,128)} %refs_0_.1), channel_id=1, source_target_pairs={{32,0},{64,32},{96,64},{128,96},{160,128},{192,160},{224,192},{256... | collective-permute-start | bytes 221192 | tf_op jit(solution)/shard_map/ppermute | solution.py:388
  7.5 0.0 collective-permute-start
  7.5 3.5 %shard_map.104 = (f32[384,128]{1,0:T(8,128)S(1)}, f32[8,128]{1,0:T(8,128)S(1)}, f32[8,128]{1,0:T(8,128)S(1)}, f32[256,128]{1,0:T(8,128)S(1)}, f32[256,128]{1,0:T...) custom-call(f32[3,3,16,128]{3,2,1,0:T(8,128)} %refs_0_.1, ...), custom_call_target="tpu_custom_call" | custom-call | tf_op jit(solution)/shard_map/pallas_call | solution.py:49
  11.0 0.0 collective-permute-done.1.right
  11.0 0.0 collective-permute-done.left
  11.0 0.2 shard_map.105
  11.1 18.3 %all_to_all.20 = f32[32,6,2,128]{3,2,1,0:T(2,128)S(1)} all-to-all(f32[32,6,2,128]{3,2,1,0:T(2,128)S(1)} %bitcast.10), channel_id=1, replica_groups=mesh['gx'=16,'gz'=16,'grp'=2] {'gz','grp'}, dimensions={0} | all-to-all | bytes 393216 | tf_op jit(solution)/shard_map/all_to_all | solution.py:381
  29.4 2.4 %shard_map.106 = f32[576,128]{1,0:T(8,128)S(1)} custom-call(f32[384,128]{1,0:T(8,128)S(1)} %bitcast.11, f32[8,128]{1,0:T(8,128)S(1)} %get-tuple-element.17.flow_row, f32[8,128]{1,0:T(8,128)S(1)} %get-tuple-element.18.slope_row, f32[256,128]{1,0:T(8,128)S(1)} %get-tuple-element.19.mask, bf16[2,256,512]{2,1,0:T(8,128)(2,1)S(1)} %get-tuple-element.20.table, ...), custom_call_target="tpu_custom_call" | custom-call | tf_op jit(solution)/shard_map/pallas_call | solution.py:49
  31.9 14.0 %all_to_all.21 = f32[32,9,2,128]{3,2,1,0:T(2,128)S(1)} all-to-all(f32[32,9,2,128]{3,2,1,0:T(2,128)S(1)} %bitcast.9), channel_id=1, replica_groups=mesh['gx'=16,'gz'=16,'grp'=2] {'gz','grp'}, dimensions={0} | all-to-all | bytes 589824 | tf_op jit(solution)/shard_map/all_to_all | solution.py:381
  45.8 1.2 %shard_map.108 = f32[3,3,16,128]{3,2,1,0:T(8,128)} custom-call(f32[576,128]{1,0:T(8,128)S(1)} %bitcast.7), custom_call_target="tpu_custom_call" | custom-call | tf_op jit(solution)/shard_map/pallas_call | solution.py:49
  47.0 24.0 %all_to_all.22.lines = f32[16,32,128]{2,1,0:T(8,128)S(1)} all-to-all(f32[16,32,128]{2,1,0:T(8,128)S(1)} %shard_map.107), channel_id=1, replica_groups=mesh['gx'=16,'gz'=16,'grp'=2] {'gx'}, dimensions={0} | all-to-all | bytes 524288 | tf_op jit(solution)/shard_map/all_to_all | solution.py:439
  71.0 1.4 %shard_map.109 = f32[288,128]{1,0:T(8,128)S(1)} custom-call(f32[16,32,128]{2,1,0:T(8,128)S(1)} %all_to_all.22.lines, f32[256,128]{1,0:T(8,128)S(1)} %get-tuple-element.26.mask, bf16[4,2,256,512]{3,2,1,0:T(8,128)(2,1)S(1)} %get-tuple-element.27.table), custom_call_target="tpu_custom_call" | custom-call | tf_op jit(solution)/shard_map/pallas_call | solution.py:49
  72.4 12.0 %all_to_all.23 = f32[16,9,2,128]{3,2,1,0:T(2,128)S(1)} all-to-all(f32[16,9,2,128]{3,2,1,0:T(2,128)S(1)} %bitcast.12), channel_id=1, replica_groups=mesh['gx'=16,'gz'=16,'grp'=2] {'gx'}, dimensions={0} | all-to-all | bytes 294912 | tf_op jit(solution)/shard_map/all_to_all | solution.py:381
  84.4 0.9 %shard_map.110 = f32[6,3,16,128]{3,2,1,0:T(8,128)} custom-call(f32[288,128]{1,0:T(8,128)S(1)} %bitcast.13), custom_call_target="tpu_custom_call" | custom-call | tf_op jit(solution)/shard_map/pallas_call | solution.py:49
  (1 shorter events, 0.0 us)
Async XLA Ops:
  0.6 10.3 %collective-permute-start.1 = (f32[3,3,16,128]{3,2,1,0:T(8,128)}, f32[3,3,16,128]{3,2,1,0:T(8,128)S(1)}, u32[]{:S(2)}, u32[]{:S(2)}) collective-permute-start(f32[3,3,16,128]{3,2,1,0:T(8,128)} %refs_0_.1), channel_id=1, source_target_pairs={{32,0},{64,32},{96,64},{128,96},{160,128},{192,160},{224,192},{256... | collective-permute-start | bytes 221192 | tf_op jit(solution)/shard_map/ppermute | solution.py:388
  7.5 3.5 %collective-permute-start = (f32[3,3,16,128]{3,2,1,0:T(8,128)}, f32[3,3,16,128]{3,2,1,0:T(8,128)S(1)}, u32[]{:S(2)}, u32[]{:S(2)}) collective-permute-start(f32[3,3,16,128]{3,2,1,0:T(8,128)} %refs_0_.1), channel_id=1, source_target_pairs={{0,32},{32,64},{64,96},{96,128},{128,160},{160,192},{192,224},{224... | collective-permute-start | bytes 221192 | tf_op jit(solution)/shard_map/ppermute | solution.py:387
